TPU v7x, 32 devices: a whole 2x2x4 slice. The times are simulated.
32 devices in a mesh: frames: 8 (over y, x, core), atoms: 4 (over z).
Axes of the slice: x: 2, y: 2, z: 4, core: 2. Of those that a mesh axis runs over, the one named last changes fastest.
Arguments:
- frames: float32 [512, 3, 6144], P('frames', None, 'atoms'), may hold values from -45 to 45, as said below
- reference_structure: float32 [3, 6144], P(None, 'atoms'), may hold values from -15 to 15
Outputs:
- covariance: float32 [3, 6144, 3, 6144], P(None, 'frames', None, 'atoms')
- mean_structure: float32 [3, 6144], P(None, 'atoms')
Inputs may be any that keep to these rules, and one draw needn't show every extreme that they name: `frames`: every frame, once centered, has a cross-covariance with the centered reference_structure of positive determinant whose singular values lie within a factor of 20 of one another.
All inputs are finite; a program needn't handle non-finite values.
Results may differ from a plain program's by a relative error of at most 0.0003.
Values may be sent and summed in bfloat16 or wider, within the bound.
No kernel may reach another device: no remote copies, remote signals or barrier semaphores. Data moves between devices by JAX's collectives and lax.ppermute only.
A program may use at most 192 MiB of HBM per device.

v0:
```python
import functools

import jax
import jax.numpy as jnp
from jax import lax
from jax.experimental import pallas as pl
from jax.experimental.pallas import tpu as pltpu
from jax.sharding import PartitionSpec as P


ITERS = 2
POLAR = 8
TILE = 256
SLOTS = 4


def polar_factor(cross):
    factor = jnp.sqrt(3.0 / jnp.sum(cross * cross, axis=(0, 1)))
    matrix = cross * factor[None, None, :]
    for _ in range(POLAR):
        entries = [[matrix[i, j] for j in range(3)] for i in range(3)]
        cofactor = [
            [
                entries[(i + 1) % 3][(j + 1) % 3] * entries[(i + 2) % 3][(j + 2) % 3]
                - entries[(i + 1) % 3][(j + 2) % 3] * entries[(i + 2) % 3][(j + 1) % 3]
                for j in range(3)
            ]
            for i in range(3)
        ]
        determinant = (
            entries[0][0] * cofactor[0][0]
            + entries[0][1] * cofactor[0][1]
            + entries[0][2] * cofactor[0][2]
        )
        inverse = jnp.stack([jnp.stack(cofactor[i]) for i in range(3)]) / determinant[None, None, :]
        matrix = 0.5 * (matrix + inverse)
    return matrix


def sum_over(value, axis, steps):
    size = lax.axis_size(axis)
    if size & (size - 1) or size > 16:
        return lax.psum(value, axis)
    for masks in steps:
        value = value + sum(lax.ppermute(value, axis, [(i, i ^ m) for i in range(size)]) for m in masks)
    return value


def powers(size):
    return [[1], range(2, size, 2)] if size > 2 else [range(1, size)]


def superpose(coords, reference_structure, atoms, count_all):
    highest = lax.Precision.HIGHEST
    count = coords.shape[1]
    mean_now = reference_structure
    for iteration in range(ITERS):
        parts = [
            jnp.einsum("cfa,da->cdf", coords, mean_now, precision=highest).reshape(9, count),
            jnp.broadcast_to(jnp.sum(mean_now, axis=1)[:, None], (3, count)),
        ]
        if iteration == 0:
            parts.append(jnp.sum(coords, axis=2))
        totals = sum_over(jnp.concatenate(parts), "atoms", [range(1, lax.axis_size("atoms"))])
        if iteration == 0:
            centroid = totals[12:15] / atoms
            shifted = coords - centroid[:, :, None]
        cross = totals[:9].reshape(3, 3, count) - centroid[:, None, :] * totals[9:12][None]
        rotation = polar_factor(cross)
        aligned = jnp.einsum("cdf,cfa->dfa", rotation, shifted, precision=highest)
        mean_now = sum_over(jnp.sum(aligned, axis=1), "frames", powers(lax.axis_size("frames"))) / count_all
    return (aligned - mean_now[:, None]).astype(jnp.bfloat16), mean_now


def product_kernel(count, scale, components, first, info, *refs):
    same, partner, row_blocks = refs[:count], refs[count : 2 * count], refs[2 * count : 3 * count]
    out, turned, ready, sent = refs[-4:]
    component, tile = pl.program_id(0), pl.program_id(1)
    step = 6 * component + tile
    slot = lax.rem(step, SLOTS)
    core, plane, is_hub = info[0], info[1], info[2]
    depth, row_count = same[0].shape[1], same[0].shape[2]

    def copy(c, d, half, k):
        start = pl.multiple_of(half * row_count, row_count)
        return pltpu.make_async_copy(
            ready.at[k], out.at[c + first, d, :, pl.ds(start, row_count)], sent.at[k]
        )

    @pl.when((tile == 0) & (is_hub == 1))
    def _():
        for s in range(count):
            turned[:, s * depth : (s + 1) * depth] = same[s][component + first].T

    @pl.when((tile == 0) & (is_hub == 0))
    def _():
        for t in range(count):
            start = pl.multiple_of((plane ^ t) * depth, depth)
            turned[:, pl.ds(start, depth)] = row_blocks[t][component].T

    @pl.when(step >= SLOTS)
    def _():
        copy(0, 0, 0, slot).wait()

    def multiply(blocks):
        right = jnp.concatenate([block[tile // 2] for block in blocks], axis=0)
        for m in range(0, row_count, TILE):
            value = jnp.dot(turned[m : m + TILE, :], right, preferred_element_type=jnp.float32)
            ready[slot, m : m + TILE, :] = value * (1.0 / scale) if scale & (scale - 1) == 0 else value / scale

    @pl.when(tile % 2 == 0)
    def _():
        multiply(same)

    @pl.when(tile % 2 == 1)
    def _():
        multiply(partner)

    copy(component, tile // 2, core ^ (tile % 2), slot).start()

    @pl.when(step == 6 * components - 1)
    def _():
        for k in range(SLOTS):
            copy(0, 0, 0, k).wait()


def covariance_part(info, first, components, same, partner, rows, count_all, so_far):
    count = len(same)
    depth, row_count = same[0].shape[1], same[0].shape[2]
    operands = [info, *same, *partner, *rows]
    specs = [pl.BlockSpec(memory_space=pltpu.SMEM)]
    specs += [pl.BlockSpec(memory_space=pltpu.VMEM)] * (3 * count)
    aliases = {}
    if so_far is not None:
        aliases = {len(operands): 0}
        operands.append(so_far)
        specs.append(pl.BlockSpec(memory_space=pl.ANY))
    return pl.pallas_call(
        functools.partial(product_kernel, count, count_all, components, first),
        out_shape=jax.ShapeDtypeStruct((3, 3, row_count, 2 * row_count), jnp.float32),
        grid=(components, 6),
        in_specs=specs,
        out_specs=pl.BlockSpec(memory_space=pl.ANY),
        scratch_shapes=[
            pltpu.VMEM((row_count, count * depth), jnp.bfloat16),
            pltpu.VMEM((SLOTS, row_count, row_count), jnp.float32),
            pltpu.SemaphoreType.DMA((SLOTS,)),
        ],
        input_output_aliases=aliases,
        compiler_params=pltpu.CompilerParams(
            dimension_semantics=("arbitrary", "arbitrary"), vmem_limit_bytes=48 * 2**20
        ),
        cost_estimate=pl.CostEstimate(
            flops=2 * count * depth * components * 6 * row_count * row_count,
            bytes_accessed=24 * components * row_count * row_count,
            transcendentals=0,
        ),
    )(*operands)


def direct(deviation, planes, row_count, count_all):
    def device(q, c, z):
        return (2 * q + c) * planes + z

    both = ("frames", "atoms")
    every = range(planes)
    swap = [(i, i ^ 1) for i in range(2 * planes)]
    place, plane = lax.axis_index("frames"), lax.axis_index("atoms")
    core = place % 2
    other = lax.ppermute(deviation, "frames", swap)
    lower = core == 0
    chip = jnp.concatenate([jnp.where(lower, deviation, other), jnp.where(lower, other, deviation)], axis=1)
    left, right = chip[:, :, :row_count], chip[:, :, row_count:]
    mine, theirs = jnp.where(lower, left, right), jnp.where(lower, right, left)
    mine, theirs, mine_early, mine_late = lax.optimization_barrier((mine, theirs, mine[:2], mine[2:]))

    def rows_of(block):
        return [
            lax.ppermute(
                block,
                both,
                [
                    (device(q ^ t ^ z, c, q), device(q, c, z))
                    for q in every
                    for c in range(2)
                    for z in every
                    if z != q
                ],
            )
            for t in every
        ]

    early = rows_of(mine_early)
    same = [mine] + [
        lax.ppermute(mine, "frames", [(2 * (q ^ s) + c, 2 * q + c) for q in every for c in range(2)])
        for s in every
        if s
    ]
    late = rows_of(mine_late)
    partner = [theirs] + [lax.ppermute(same[s], "frames", swap) for s in every if s]
    info = jnp.stack([core, plane, (place // 2 == plane).astype(jnp.int32)]).astype(jnp.int32)
    product = covariance_part(info, 0, 2, same, partner, early, count_all, None)
    product = covariance_part(info, 2, 1, same, partner, late, count_all, product)
    return jnp.transpose(product, (0, 2, 1, 3))


def permutes_fit(planes, places):
    return places == 2 * planes and planes <= 4 and planes & (planes - 1) == 0


def general(deviation, row_count, count_all):
    panel = lax.all_gather(deviation, "frames", axis=1, tiled=True)
    ratio = lax.axis_size("frames") // lax.axis_size("atoms")
    place = lax.axis_index("frames")
    selected = lax.dynamic_slice_in_dim(panel, place % ratio * row_count, row_count, 2)
    mine = lax.axis_index("atoms") == place // ratio
    rows = lax.psum(jnp.where(mine, selected, jnp.zeros_like(selected)), "atoms")
    product = jnp.einsum("cfa,dfb->cadb", rows, panel, preferred_element_type=jnp.float32)
    return product / count_all


def whole(frames, reference_structure):
    coords = jnp.transpose(frames, (1, 0, 2))
    planes, places = lax.axis_size("atoms"), lax.axis_size("frames")
    column_atoms = frames.shape[2]
    atoms = column_atoms * planes
    count_all = frames.shape[0] * places
    row_count = atoms // places
    deviation, mean = superpose(coords, reference_structure, atoms, count_all)
    if permutes_fit(planes, places) and row_count % TILE == 0:
        covariance = direct(deviation, planes, row_count, count_all)
    else:
        covariance = general(deviation, row_count, count_all)
    return covariance, mean


def solution(mesh):
    return jax.shard_map(
        whole,
        mesh=mesh,
        in_specs=(P("frames", None, "atoms"), P(None, "atoms")),
        out_specs=(P(None, "frames", None, "atoms"), P(None, "atoms")),
        check_vma=False,
    )
```

profile of v0, /device:TPU:0, one launch (start us, length us, event | category | flops | bytes accessed | tf_op | source)
XLA Modules:
  0.0 168.7 jit_solution(10263491153403085606)
XLA Ops:
  0.7 1.5 bitcast_reduce_fusion.1
  2.2 0.1 copy-done.6
  2.3 2.0 %fusion.7 = f32[3,3,64]{2,1,0:T(4,128)S(1)} fusion(f32[64,3,1536]{2,0,1:T(8,128)S(1)} %copy-done.6, f32[3,1536]{1,0:T(4,128)} %param.3), kind=kOutput, calls=%fused_computation.14 | convolution fusion | flops 10616832 | bytes 1200384 | tf_op jit(solution)/shard_map/cfa,da->cdf/dot_general | solution.py:59
  4.3 0.1 reduce_sum.58
  4.6 5.1 %collective-permute-start.2 = (f32[15,64]{1,0:T(8,128)S(1)}, f32[15,64]{1,0:T(8,128)S(1)}, u32[]{:S(2)}, u32[]{:S(2)}) collective-permute-start(f32[15,64]{1,0:T(8,128)S(1)} %pad_maximum_fusion.1), channel_id=1, source_target_pairs={{0,3},{1,2},{2,1},{3,0},{4,7},{5,6},{6,5},{7,4},{8,11},{9,10},{10,... | collective-permute-start | bytes 11528 | tf_op jit(solution)/shard_map/ppermute | solution.py:45
  9.7 0.6 collective-permute-start
  10.3 1.0 collective-permute-done.2
  11.3 2.9 %collective-permute-done.1 = f32[15,64]{1,0:T(8,128)S(1)} collective-permute-done((f32[15,64]{1,0:T(8,128)S(1)}, f32[15,64]{1,0:T(8,128)S(1)}, u32[]{:S(2)}, u32[]{:S(2)}) %collective-permute-start.1) | collective-permute-done | bytes 3872 | tf_op jit(solution)/shard_map/ppermute | solution.py:45
  15.2 0.1 bitcast_subtract_fusion.1
  15.4 0.7 convolution_bitcast_fusion
  16.2 1.2 collective-permute-done.3
  17.4 2.5 %collective-permute-start.6 = (f32[3,1536]{1,0:T(4,128)S(1)}, f32[3,1536]{1,0:T(4,128)S(1)}, u32[]{:S(2)}, u32[]{:S(2)}) collective-permute-start(f32[3,1536]{1,0:T(4,128)S(1)} %add.251), channel_id=1, source_target_pairs={{0,24},{4,28},{8,16},{12,20},{16,8},{20,12},{24,0},{28,4},{1,25},{... | collective-permute-start | bytes 55304 | tf_op jit(solution)/shard_map/ppermute | solution.py:45
  19.9 0.5 collective-permute-start.5
  20.4 0.5 collective-permute-start.4
  20.9 1.2 collective-permute-done.6
  22.2 1.5 collective-permute-done.5
  23.7 0.5 collective-permute-done.4
  24.2 0.1 fusion.36
  24.3 0.1 pad.99.clone
  24.4 1.3 fusion.10
  25.8 1.5 collective-permute-start.9
  27.3 0.6 collective-permute-start.8
  27.9 2.3 %collective-permute-start.7 = (f32[12,64]{1,0:T(8,128)S(1)}, f32[12,64]{1,0:T(8,128)S(1)}, u32[]{:S(2)}, u32[]{:S(2)}) collective-permute-start(f32[12,64]{1,0:T(8,128)S(1)} %pad_maximum_fusion.2), channel_id=1, source_target_pairs={{0,1},{1,0},{2,3},{3,2},{4,5},{5,4},{6,7},{7,6},{8,9},{9,8},{10,11... | collective-permute-start | bytes 9224 | tf_op jit(solution)/shard_map/ppermute | solution.py:45
  30.2 1.1 collective-permute-done.9
  31.3 0.6 collective-permute-done.8
  31.9 0.1 collective-permute-done.7
  33.1 0.1 copy.6
  33.2 3.4 %fusion = f32[64,1536,3]{1,2,0:T(4,128)S(1)} fusion(f32[3,3,64]{0,1,2:T(4,128)S(1)} %copy.6, f32[3,64,1536]{2,1,0:T(8,128)S(1)} %bitcast_subtract_fusion.1), kind=kOutput, calls=%fused_computation.1 | convolution fusion | flops 10616832 | bytes 2361600 | tf_op jit(solution)/shard_map/cdf,cfa->dfa/dot_general | solution.py:70
  36.7 0.4 bitcast_reduce_fusion
  37.1 1.2 collective-permute-done.10
  38.3 1.6 collective-permute-start.13
  39.8 0.5 collective-permute-start.12
  40.4 1.5 collective-permute-start.11
  41.8 1.2 collective-permute-done.13
  43.1 0.6 collective-permute-done.12
  43.7 0.5 collective-permute-done.11
  44.2 0.3 fusion.2
  44.7 2.0 %collective-permute-done.14 = bf16[3,64,1536]{2,1,0:T(8,128)(2,1)S(1)} collective-permute-done((bf16[3,64,1536]{2,1,0:T(8,128)(2,1)S(1)}, bf16[3,64,1536]{2,1,0:T(8,128)(2,1)S(1)}, u32[]{:S(2)}, u32[]{:S(2)}) %collective-permute-start.14) | collective-permute-done | bytes 589856 | tf_op jit(solution)/shard_map/ppermute | solution.py:170
  46.6 0.4 broadcast_select_fusion.1
  47.0 0.2 broadcast_select_fusion.2
  47.2 0.7 slice.764
  47.9 0.8 slice.763
  48.7 2.4 %collective-permute-start.17 = (bf16[3,128,768]{2,1,0:T(8,128)(2,1)S(1)}, bf16[3,128,768]{2,1,0:T(8,128)(2,1)S(1)}, u32[]{:S(2)}, u32[]{:S(2)}) collective-permute-start(bf16[3,128,768]{2,1,0:T(8,128)(2,1)S(1)} %get-tuple-element.6.refs_0_), channel_id=1, source_target_pairs={{24,0},{28,4},{16,8},{20,12},{8,16},{12,20},{0,24},{4,28},{25,1},{... | collective-permute-start | bytes 1769480 | tf_op jit(solution)/shard_map/ppermute | solution.py:195
  51.1 0.5 collective-permute-start.16
  51.7 0.5 collective-permute-start.15
  52.2 4.4 %collective-permute-start.28 = (bf16[2,128,768]{2,1,0:T(8,128)(2,1)}, bf16[2,128,768]{2,1,0:T(8,128)(2,1)S(1)}, u32[]{:S(2)}, u32[]{:S(2)}) collective-permute-start(bf16[2,128,768]{2,1,0:T(8,128)(2,1)} %slice.763), channel_id=1, source_target_pairs={{16,1},{8,2},{0,3},{20,5},{12,6},{4,7},{17,8},{1,10},{9,11},{21,12... | collective-permute-start | bytes 1179656 | tf_op jit(solution)/shard_map/ppermute | solution.py:179
  56.6 3.8 %collective-permute-start.27 = (bf16[2,128,768]{2,1,0:T(8,128)(2,1)}, bf16[2,128,768]{2,1,0:T(8,128)(2,1)S(1)}, u32[]{:S(2)}, u32[]{:S(2)}) collective-permute-start(bf16[2,128,768]{2,1,0:T(8,128)(2,1)} %slice.763), channel_id=1, source_target_pairs={{24,1},{0,2},{8,3},{28,5},{4,6},{12,7},{25,8},{9,10},{1,11},{29,12... | collective-permute-start | bytes 1179656 | tf_op jit(solution)/shard_map/ppermute | solution.py:179
  60.4 13.2 %collective-permute-done.17.refs_3_ = bf16[3,128,768]{2,1,0:T(8,128)(2,1)S(1)} collective-permute-done((bf16[3,128,768]{2,1,0:T(8,128)(2,1)S(1)}, bf16[3,128,768]{2,1,0:T(8,128)(2,1)S(1)}, u32[]{:S(2)}, u32[]{:S(2)}) %collective-permute-start.17) | collective-permute-done | bytes 589856 | tf_op jit(solution)/shard_map/ppermute | solution.py:195
  73.6 19.9 %collective-permute-done.16.refs_2_ = bf16[3,128,768]{2,1,0:T(8,128)(2,1)S(1)} collective-permute-done((bf16[3,128,768]{2,1,0:T(8,128)(2,1)S(1)}, bf16[3,128,768]{2,1,0:T(8,128)(2,1)S(1)}, u32[]{:S(2)}, u32[]{:S(2)}) %collective-permute-start.16) | collective-permute-done | bytes 589856 | tf_op jit(solution)/shard_map/ppermute | solution.py:195
  93.5 0.5 collective-permute-start.18
  94.0 0.7 copy-done.2
  94.8 5.6 %collective-permute-start.26 = (bf16[2,128,768]{2,1,0:T(8,128)(2,1)}, bf16[2,128,768]{2,1,0:T(8,128)(2,1)}, u32[]{:S(2)}, u32[]{:S(2)}) collective-permute-start(bf16[2,128,768]{2,1,0:T(8,128)(2,1)} %slice.763), channel_id=1, source_target_pairs={{0,1},{24,2},{16,3},{4,5},{28,6},{20,7},{1,8},{17,10},{25,11},{5,1... | collective-permute-start | bytes 1179656 | tf_op jit(solution)/shard_map/ppermute | solution.py:179
  100.3 0.7 copy-done.4
  101.1 1.4 collective-permute-start.25
  102.5 5.9 %collective-permute-done.26.refs_9_ = bf16[2,128,768]{2,1,0:T(8,128)(2,1)} collective-permute-done((bf16[2,128,768]{2,1,0:T(8,128)(2,1)}, bf16[2,128,768]{2,1,0:T(8,128)(2,1)}, u32[]{:S(2)}, u32[]{:S(2)}) %collective-permute-start.26) | collective-permute-done | bytes 393248 | tf_op jit(solution)/shard_map/ppermute | solution.py:179
  108.4 6.3 %collective-permute-start.24 = (bf16[1,128,768]{2,1,0:T(8,128)(2,1)}, bf16[1,128,768]{2,1,0:T(8,128)(2,1)S(1)}, u32[]{:S(2)}, u32[]{:S(2)}) collective-permute-start(bf16[1,128,768]{2,1,0:T(8,128)(2,1)} %slice.764), channel_id=1, source_target_pairs={{16,1},{8,2},{0,3},{20,5},{12,6},{4,7},{17,8},{1,10},{9,11},{21,12... | collective-permute-start | bytes 589832 | tf_op jit(solution)/shard_map/ppermute | solution.py:179
  114.7 20.0 %collective-permute-start.23 = (bf16[1,128,768]{2,1,0:T(8,128)(2,1)}, bf16[1,128,768]{2,1,0:T(8,128)(2,1)S(1)}, u32[]{:S(2)}, u32[]{:S(2)}) collective-permute-start(bf16[1,128,768]{2,1,0:T(8,128)(2,1)} %slice.764), channel_id=1, source_target_pairs={{24,1},{0,2},{8,3},{28,5},{4,6},{12,7},{25,8},{9,10},{1,11},{29,12... | collective-permute-start | bytes 589832 | tf_op jit(solution)/shard_map/ppermute | solution.py:179
  134.8 7.9 %collective-permute-start.22 = (bf16[1,128,768]{2,1,0:T(8,128)(2,1)}, bf16[1,128,768]{2,1,0:T(8,128)(2,1)S(1)}, u32[]{:S(2)}, u32[]{:S(2)}) collective-permute-start(bf16[1,128,768]{2,1,0:T(8,128)(2,1)} %slice.764), channel_id=1, source_target_pairs={{0,1},{24,2},{16,3},{4,5},{28,6},{20,7},{1,8},{17,10},{25,11},{5,1... | collective-permute-start | bytes 589832 | tf_op jit(solution)/shard_map/ppermute | solution.py:179
  142.7 0.9 collective-permute-start.21
  143.6 1.0 copy-done.3
  144.6 1.0 copy-done.5
  145.6 13.8 %shard_map.41.refs_12_ = f32[3,3,768,1536]{3,2,1,0:T(8,128)} custom-call(s32[3]{0:T(128)S(1)} %pad_add_fusion.info, bf16[3,128,768]{2,1,0:T(8,128)(2,1)S(1)} %get-tuple-element.6.refs_0_, bf16[3,128,768]{2,1,0:T(8,128)(2,1)S(1)} %collective-permute-done.15.refs_1_, bf16[3,128,768]{2,1,0:T(8,128)(2,1)S(1)} %collective-permute-done.16.refs_2_, ...), custom_call_target="tpu_custom_call" | custom-call | flops 7247757312 | bytes 28311552 | tf_op jit(solution)/shard_map/pallas_call | solution.py:138
  159.4 1.1 copy-done.1
  160.5 8.0 %shard_map.42 = f32[3,3,768,1536]{3,2,1,0:T(8,128)} custom-call(s32[3]{0:T(128)S(1)} %pad_add_fusion.info, bf16[3,128,768]{2,1,0:T(8,128)(2,1)S(1)} %get-tuple-element.6.refs_0_, bf16[3,128,768]{2,1,0:T(8,128)(2,1)S(1)} %collective-permute-done.15.refs_1_, bf16[3,128,768]{2,1,0:T(8,128)(2,1)S(1)} %collective-permute-done.16.refs_2_, ...), custom_call_target="tpu_custom_call", output_to_operand_aliasing={{}: (13, {})} | custom-call | flops 3623878656 | bytes 14155776 | tf_op jit(solution)/shard_map/pallas_call | solution.py:138
  (149 shorter events, 2.2 us)
Async XLA Ops:
  0.6 1.6 copy-start.6
  0.6 3.7 %copy-start.8 = (f32[3,1536]{1,0:T(4,128)S(1)}, f32[3,1536]{1,0:T(4,128)}, u32[]{:S(2)}) copy-start(f32[3,1536]{1,0:T(4,128)} %param.3) | copy-start | bytes 55300
  4.6 6.7 %collective-permute-start.2 = (f32[15,64]{1,0:T(8,128)S(1)}, f32[15,64]{1,0:T(8,128)S(1)}, u32[]{:S(2)}, u32[]{:S(2)}) collective-permute-start(f32[15,64]{1,0:T(8,128)S(1)} %pad_maximum_fusion.1), channel_id=1, source_target_pairs={{0,3},{1,2},{2,1},{3,0},{4,7},{5,6},{6,5},{7,4},{8,11},{9,10},{10,... | collective-permute-start | bytes 11528 | tf_op jit(solution)/shard_map/ppermute | solution.py:45
  9.7 4.5 %collective-permute-start.1 = (f32[15,64]{1,0:T(8,128)S(1)}, f32[15,64]{1,0:T(8,128)S(1)}, u32[]{:S(2)}, u32[]{:S(2)}) collective-permute-start(f32[15,64]{1,0:T(8,128)S(1)} %pad_maximum_fusion.1), channel_id=1, source_target_pairs={{0,2},{1,3},{2,0},{3,1},{4,6},{5,7},{6,4},{7,5},{8,10},{9,11},{10,... | collective-permute-start | bytes 11528 | tf_op jit(solution)/shard_map/ppermute | solution.py:45
  9.7 4.5 %collective-permute-start = (f32[15,64]{1,0:T(8,128)S(1)}, f32[15,64]{1,0:T(8,128)S(1)}, u32[]{:S(2)}, u32[]{:S(2)}) collective-permute-start(f32[15,64]{1,0:T(8,128)S(1)} %pad_maximum_fusion.1), channel_id=1, source_target_pairs={{0,1},{1,0},{2,3},{3,2},{4,5},{5,4},{6,7},{7,6},{8,9},{9,8},{10,11... | collective-permute-start | bytes 11528 | tf_op jit(solution)/shard_map/ppermute | solution.py:45
  16.1 1.3 collective-permute-start.3
  17.4 4.8 %collective-permute-start.6 = (f32[3,1536]{1,0:T(4,128)S(1)}, f32[3,1536]{1,0:T(4,128)S(1)}, u32[]{:S(2)}, u32[]{:S(2)}) collective-permute-start(f32[3,1536]{1,0:T(4,128)S(1)} %add.251), channel_id=1, source_target_pairs={{0,24},{4,28},{8,16},{12,20},{16,8},{20,12},{24,0},{28,4},{1,25},{... | collective-permute-start | bytes 55304 | tf_op jit(solution)/shard_map/ppermute | solution.py:45
  19.9 3.8 %collective-permute-start.5 = (f32[3,1536]{1,0:T(4,128)S(1)}, f32[3,1536]{1,0:T(4,128)S(1)}, u32[]{:S(2)}, u32[]{:S(2)}) collective-permute-start(f32[3,1536]{1,0:T(4,128)S(1)} %add.251), channel_id=1, source_target_pairs={{0,16},{4,20},{8,24},{12,28},{16,0},{20,4},{24,8},{28,12},{1,17},{... | collective-permute-start | bytes 55304 | tf_op jit(solution)/shard_map/ppermute | solution.py:45
  20.4 3.8 %collective-permute-start.4 = (f32[3,1536]{1,0:T(4,128)S(1)}, f32[3,1536]{1,0:T(4,128)S(1)}, u32[]{:S(2)}, u32[]{:S(2)}) collective-permute-start(f32[3,1536]{1,0:T(4,128)S(1)} %add.251), channel_id=1, source_target_pairs={{0,8},{4,12},{8,0},{12,4},{16,24},{20,28},{24,16},{28,20},{1,9},{5... | collective-permute-start | bytes 55304 | tf_op jit(solution)/shard_map/ppermute | solution.py:45
  25.8 5.5 %collective-permute-start.9 = (f32[12,64]{1,0:T(8,128)S(1)}, f32[12,64]{1,0:T(8,128)S(1)}, u32[]{:S(2)}, u32[]{:S(2)}) collective-permute-start(f32[12,64]{1,0:T(8,128)S(1)} %pad_maximum_fusion.2), channel_id=1, source_target_pairs={{0,3},{1,2},{2,1},{3,0},{4,7},{5,6},{6,5},{7,4},{8,11},{9,10},{10,... | collective-permute-start | bytes 9224 | tf_op jit(solution)/shard_map/ppermute | solution.py:45
  27.3 4.6 %collective-permute-start.8 = (f32[12,64]{1,0:T(8,128)S(1)}, f32[12,64]{1,0:T(8,128)S(1)}, u32[]{:S(2)}, u32[]{:S(2)}) collective-permute-start(f32[12,64]{1,0:T(8,128)S(1)} %pad_maximum_fusion.2), channel_id=1, source_target_pairs={{0,2},{1,3},{2,0},{3,1},{4,6},{5,7},{6,4},{7,5},{8,10},{9,11},{10,... | collective-permute-start | bytes 9224 | tf_op jit(solution)/shard_map/ppermute | solution.py:45
  27.9 4.0 %collective-permute-start.7 = (f32[12,64]{1,0:T(8,128)S(1)}, f32[12,64]{1,0:T(8,128)S(1)}, u32[]{:S(2)}, u32[]{:S(2)}) collective-permute-start(f32[12,64]{1,0:T(8,128)S(1)} %pad_maximum_fusion.2), channel_id=1, source_target_pairs={{0,1},{1,0},{2,3},{3,2},{4,5},{5,4},{6,7},{7,6},{8,9},{9,8},{10,11... | collective-permute-start | bytes 9224 | tf_op jit(solution)/shard_map/ppermute | solution.py:45
  37.0 1.3 collective-permute-start.10
  38.3 4.8 %collective-permute-start.13 = (f32[3,1536]{1,0:T(4,128)S(1)}, f32[3,1536]{1,0:T(4,128)S(1)}, u32[]{:S(2)}, u32[]{:S(2)}) collective-permute-start(f32[3,1536]{1,0:T(4,128)S(1)} %add.282), channel_id=1, source_target_pairs={{0,24},{4,28},{8,16},{12,20},{16,8},{20,12},{24,0},{28,4},{1,25},{... | collective-permute-start | bytes 55304 | tf_op jit(solution)/shard_map/ppermute | solution.py:45
  39.8 3.8 %collective-permute-start.12 = (f32[3,1536]{1,0:T(4,128)S(1)}, f32[3,1536]{1,0:T(4,128)S(1)}, u32[]{:S(2)}, u32[]{:S(2)}) collective-permute-start(f32[3,1536]{1,0:T(4,128)S(1)} %add.282), channel_id=1, source_target_pairs={{0,16},{4,20},{8,24},{12,28},{16,0},{20,4},{24,8},{28,12},{1,17},{... | collective-permute-start | bytes 55304 | tf_op jit(solution)/shard_map/ppermute | solution.py:45
  40.4 3.8 %collective-permute-start.11 = (f32[3,1536]{1,0:T(4,128)S(1)}, f32[3,1536]{1,0:T(4,128)S(1)}, u32[]{:S(2)}, u32[]{:S(2)}) collective-permute-start(f32[3,1536]{1,0:T(4,128)S(1)} %add.282), channel_id=1, source_target_pairs={{0,8},{4,12},{8,0},{12,4},{16,24},{20,28},{24,16},{28,20},{1,9},{5... | collective-permute-start | bytes 55304 | tf_op jit(solution)/shard_map/ppermute | solution.py:45
  44.2 2.8 %copy-start.7 = (f32[3,1536]{1,0:T(4,128)}, f32[3,1536]{1,0:T(4,128)S(1)}, u32[]{:S(2)}) copy-start(f32[3,1536]{1,0:T(4,128)S(1)} %add_multiply_fusion) | copy-start | bytes 55300
  44.6 2.1 %collective-permute-start.14 = (bf16[3,64,1536]{2,1,0:T(8,128)(2,1)S(1)}, bf16[3,64,1536]{2,1,0:T(8,128)(2,1)S(1)}, u32[]{:S(2)}, u32[]{:S(2)}) collective-permute-start(bf16[3,64,1536]{2,1,0:T(8,128)(2,1)S(1)} %fusion.2), channel_id=1, source_target_pairs={{0,4},{4,0},{8,12},{12,8},{16,20},{20,16},{24,28},{28,24},{1,5},{5... | collective-permute-start | bytes 1769480 | tf_op jit(solution)/shard_map/ppermute | solution.py:170
  48.7 24.9 %collective-permute-start.17 = (bf16[3,128,768]{2,1,0:T(8,128)(2,1)S(1)}, bf16[3,128,768]{2,1,0:T(8,128)(2,1)S(1)}, u32[]{:S(2)}, u32[]{:S(2)}) collective-permute-start(bf16[3,128,768]{2,1,0:T(8,128)(2,1)S(1)} %get-tuple-element.6.refs_0_), channel_id=1, source_target_pairs={{24,0},{28,4},{16,8},{20,12},{8,16},{12,20},{0,24},{4,28},{25,1},{... | collective-permute-start | bytes 1769480 | tf_op jit(solution)/shard_map/ppermute | solution.py:195
  51.1 42.4 %collective-permute-start.16 = (bf16[3,128,768]{2,1,0:T(8,128)(2,1)S(1)}, bf16[3,128,768]{2,1,0:T(8,128)(2,1)S(1)}, u32[]{:S(2)}, u32[]{:S(2)}) collective-permute-start(bf16[3,128,768]{2,1,0:T(8,128)(2,1)S(1)} %get-tuple-element.6.refs_0_), channel_id=1, source_target_pairs={{16,0},{20,4},{24,8},{28,12},{0,16},{4,20},{8,24},{12,28},{17,1},{... | collective-permute-start | bytes 1769480 | tf_op jit(solution)/shard_map/ppermute | solution.py:195
  51.7 41.9 %collective-permute-start.15 = (bf16[3,128,768]{2,1,0:T(8,128)(2,1)S(1)}, bf16[3,128,768]{2,1,0:T(8,128)(2,1)S(1)}, u32[]{:S(2)}, u32[]{:S(2)}) collective-permute-start(bf16[3,128,768]{2,1,0:T(8,128)(2,1)S(1)} %get-tuple-element.6.refs_0_), channel_id=1, source_target_pairs={{8,0},{12,4},{0,8},{4,12},{24,16},{28,20},{16,24},{20,28},{9,1},{1... | collective-permute-start | bytes 1769480 | tf_op jit(solution)/shard_map/ppermute | solution.py:195
  52.2 41.8 %collective-permute-start.28 = (bf16[2,128,768]{2,1,0:T(8,128)(2,1)}, bf16[2,128,768]{2,1,0:T(8,128)(2,1)S(1)}, u32[]{:S(2)}, u32[]{:S(2)}) collective-permute-start(bf16[2,128,768]{2,1,0:T(8,128)(2,1)} %slice.763), channel_id=1, source_target_pairs={{16,1},{8,2},{0,3},{20,5},{12,6},{4,7},{17,8},{1,10},{9,11},{21,12... | collective-permute-start | bytes 1179656 | tf_op jit(solution)/shard_map/ppermute | solution.py:179
  56.6 43.7 %collective-permute-start.27 = (bf16[2,128,768]{2,1,0:T(8,128)(2,1)}, bf16[2,128,768]{2,1,0:T(8,128)(2,1)S(1)}, u32[]{:S(2)}, u32[]{:S(2)}) collective-permute-start(bf16[2,128,768]{2,1,0:T(8,128)(2,1)} %slice.763), channel_id=1, source_target_pairs={{24,1},{0,2},{8,3},{28,5},{4,6},{12,7},{25,8},{9,10},{1,11},{29,12... | collective-permute-start | bytes 1179656 | tf_op jit(solution)/shard_map/ppermute | solution.py:179
  73.6 61.1 %collective-permute-start.20 = (bf16[3,128,768]{2,1,0:T(8,128)(2,1)S(1)}, bf16[3,128,768]{2,1,0:T(8,128)(2,1)S(1)}, u32[]{:S(2)}, u32[]{:S(2)}) collective-permute-start(bf16[3,128,768]{2,1,0:T(8,128)(2,1)S(1)} %collective-permute-done.17.refs_3_), channel_id=1, source_target_pairs={{0,4},{4,0},{8,12},{12,8},{16,20},{20,16},{24,28},{28,24},{1,5},{5... | collective-permute-start | bytes 1769480 | tf_op jit(solution)/shard_map/ppermute | solution.py:200
  93.5 49.2 %collective-permute-start.19 = (bf16[3,128,768]{2,1,0:T(8,128)(2,1)S(1)}, bf16[3,128,768]{2,1,0:T(8,128)(2,1)}, u32[]{:S(2)}, u32[]{:S(2)}) collective-permute-start(bf16[3,128,768]{2,1,0:T(8,128)(2,1)S(1)} %collective-permute-done.16.refs_2_), channel_id=1, source_target_pairs={{0,4},{4,0},{8,12},{12,8},{16,20},{20,16},{24,28},{28,24},{1,5},{5... | collective-permute-start | bytes 1769480 | tf_op jit(solution)/shard_map/ppermute | solution.py:200
  93.5 50.0 %collective-permute-start.18 = (bf16[3,128,768]{2,1,0:T(8,128)(2,1)S(1)}, bf16[3,128,768]{2,1,0:T(8,128)(2,1)}, u32[]{:S(2)}, u32[]{:S(2)}) collective-permute-start(bf16[3,128,768]{2,1,0:T(8,128)(2,1)S(1)} %collective-permute-done.15.refs_1_), channel_id=1, source_target_pairs={{0,4},{4,0},{8,12},{12,8},{16,20},{20,16},{24,28},{28,24},{1,5},{5... | collective-permute-start | bytes 1769480 | tf_op jit(solution)/shard_map/ppermute | solution.py:200
  94.0 0.7 copy-start.2
  94.8 13.7 %collective-permute-start.26 = (bf16[2,128,768]{2,1,0:T(8,128)(2,1)}, bf16[2,128,768]{2,1,0:T(8,128)(2,1)}, u32[]{:S(2)}, u32[]{:S(2)}) collective-permute-start(bf16[2,128,768]{2,1,0:T(8,128)(2,1)} %slice.763), channel_id=1, source_target_pairs={{0,1},{24,2},{16,3},{4,5},{28,6},{20,7},{1,8},{17,10},{25,11},{5,1... | collective-permute-start | bytes 1179656 | tf_op jit(solution)/shard_map/ppermute | solution.py:179
  100.3 0.7 copy-start.4
  101.1 13.6 %collective-permute-start.25 = (bf16[2,128,768]{2,1,0:T(8,128)(2,1)}, bf16[2,128,768]{2,1,0:T(8,128)(2,1)}, u32[]{:S(2)}, u32[]{:S(2)}) collective-permute-start(bf16[2,128,768]{2,1,0:T(8,128)(2,1)} %slice.763), channel_id=1, source_target_pairs={{8,1},{16,2},{24,3},{12,5},{20,6},{28,7},{9,8},{25,10},{17,11},{13... | collective-permute-start | bytes 1179656 | tf_op jit(solution)/shard_map/ppermute | solution.py:179
  108.4 51.0 %collective-permute-start.24 = (bf16[1,128,768]{2,1,0:T(8,128)(2,1)}, bf16[1,128,768]{2,1,0:T(8,128)(2,1)S(1)}, u32[]{:S(2)}, u32[]{:S(2)}) collective-permute-start(bf16[1,128,768]{2,1,0:T(8,128)(2,1)} %slice.764), channel_id=1, source_target_pairs={{16,1},{8,2},{0,3},{20,5},{12,6},{4,7},{17,8},{1,10},{9,11},{21,12... | collective-permute-start | bytes 589832 | tf_op jit(solution)/shard_map/ppermute | solution.py:179
  114.7 44.7 %collective-permute-start.23 = (bf16[1,128,768]{2,1,0:T(8,128)(2,1)}, bf16[1,128,768]{2,1,0:T(8,128)(2,1)S(1)}, u32[]{:S(2)}, u32[]{:S(2)}) collective-permute-start(bf16[1,128,768]{2,1,0:T(8,128)(2,1)} %slice.764), channel_id=1, source_target_pairs={{24,1},{0,2},{8,3},{28,5},{4,6},{12,7},{25,8},{9,10},{1,11},{29,12... | collective-permute-start | bytes 589832 | tf_op jit(solution)/shard_map/ppermute | solution.py:179
  134.7 8.8 %copy-start = (bf16[3,128,768]{2,1,0:T(8,128)(2,1)}, bf16[3,128,768]{2,1,0:T(8,128)(2,1)S(1)}, u32[]{:S(2)}) copy-start(bf16[3,128,768]{2,1,0:T(8,128)(2,1)S(1)} %collective-permute-done.20.refs_7_) | copy-start | bytes 1769476
  134.8 24.7 %collective-permute-start.22 = (bf16[1,128,768]{2,1,0:T(8,128)(2,1)}, bf16[1,128,768]{2,1,0:T(8,128)(2,1)S(1)}, u32[]{:S(2)}, u32[]{:S(2)}) collective-permute-start(bf16[1,128,768]{2,1,0:T(8,128)(2,1)} %slice.764), channel_id=1, source_target_pairs={{0,1},{24,2},{16,3},{4,5},{28,6},{20,7},{1,8},{17,10},{25,11},{5,1... | collective-permute-start | bytes 589832 | tf_op jit(solution)/shard_map/ppermute | solution.py:179
  142.7 16.7 %collective-permute-start.21 = (bf16[1,128,768]{2,1,0:T(8,128)(2,1)}, bf16[1,128,768]{2,1,0:T(8,128)(2,1)S(1)}, u32[]{:S(2)}, u32[]{:S(2)}) collective-permute-start(bf16[1,128,768]{2,1,0:T(8,128)(2,1)} %slice.764), channel_id=1, source_target_pairs={{8,1},{16,2},{24,3},{12,5},{20,6},{28,7},{9,8},{25,10},{17,11},{13... | collective-permute-start | bytes 589832 | tf_op jit(solution)/shard_map/ppermute | solution.py:179
  143.6 1.0 copy-start.3
  144.6 1.0 copy-start.5
  159.4 1.1 copy-start.1
where the time goes:
time: 170 us; the launch traced here: 169 us
  starting transfers between devices  71.7 us (42%)
  waiting for transfers between devices  54.6 us (32%)
  Pallas kernels  21.8 us (13%)
  matrix products  7.45 us (4%)
  local copies, waits for them, and re-layouts  6.46 us (4%)
  other arithmetic  4.92 us (3%)
  between operations  1.79 us (1%)
    ppermute x8, starting transfers between devices, rows_of(): lax.ppermute(block, both, [(device(q ^ t ^ z, c, q), device(q, c, z)) for...  50.2 us
    ppermute x3, waiting for transfers between devices, direct(): lax.ppermute(mine, 'frames', [(2 * (q ^ s) + c, 2 * q + c) for q in every...  33.1 us
    pallas_call x2, Pallas kernels, covariance_part(): pl.pallas_call(functools.partial(product_kernel, count, count_all, compon...  21.8 us
    ppermute x14, starting transfers between devices, sum_over(): lax.ppermute(value, axis, [(i, i ^ m) for i in range(size)])  17.4 us
    ppermute x14, waiting for transfers between devices, sum_over(): lax.ppermute(value, axis, [(i, i ^ m) for i in range(size)])  13.6 us
    ppermute x8, waiting for transfers between devices, rows_of(): lax.ppermute(block, both, [(device(q ^ t ^ z, c, q), device(q, c, z)) for...  5.89 us
    unnamed x18, local copies, waits for them, and re-layouts  4.64 us
    dot_general x2, matrix products, superpose(): aligned = jnp.einsum('cdf,cfa->dfa', rotation, shifted, precision=highest)  4.09 us
  transfers between devices with their start and end apart: 29, of which 17 were waited for; matrix products, arithmetic and copies ran while one was open for 0% of the time, Pallas kernels for 8%

commit v1 on v0

--- a/solution.py
+++ b/solution.py
@@ -12,6 +12,7 @@
 POLAR = 8
 TILE = 256
 SLOTS = 4
+EARLY = 1
 
 
 def polar_factor(cross):
@@ -55,19 +56,23 @@
     count = coords.shape[1]
     mean_now = reference_structure
     for iteration in range(ITERS):
-        parts = [
-            jnp.einsum("cfa,da->cdf", coords, mean_now, precision=highest).reshape(9, count),
-            jnp.broadcast_to(jnp.sum(mean_now, axis=1)[:, None], (3, count)),
-        ]
+        weights = mean_now
         if iteration == 0:
-            parts.append(jnp.sum(coords, axis=2))
+            weights = jnp.concatenate([mean_now, jnp.ones_like(mean_now[:1])])
+        sums = jnp.einsum("cfa,da->dcf", coords, weights, precision=highest).reshape(-1, count)
+        parts = [sums, jnp.broadcast_to(jnp.sum(mean_now, axis=1)[:, None], (3, count))]
         totals = sum_over(jnp.concatenate(parts), "atoms", [range(1, lax.axis_size("atoms"))])
         if iteration == 0:
-            centroid = totals[12:15] / atoms
+            centroid = totals[9:12] / atoms
             shifted = coords - centroid[:, :, None]
-        cross = totals[:9].reshape(3, 3, count) - centroid[:, None, :] * totals[9:12][None]
+        cross = totals[:9].reshape(3, 3, count).transpose(1, 0, 2) - centroid[:, None, :] * totals[-3:][None]
         rotation = polar_factor(cross)
-        aligned = jnp.einsum("cdf,cfa->dfa", rotation, shifted, precision=highest)
+        if iteration == ITERS - 1:
+            aligned = jnp.stack(
+                [sum(rotation[c, d][:, None] * shifted[c] for c in range(3)) for d in range(3)]
+            )
+        else:
+            aligned = jnp.einsum("cdf,cfa->dfa", rotation, shifted, precision=highest)
         mean_now = sum_over(jnp.sum(aligned, axis=1), "frames", powers(lax.axis_size("frames"))) / count_all
     return (aligned - mean_now[:, None]).astype(jnp.bfloat16), mean_now
 
@@ -81,10 +86,12 @@
     core, plane, is_hub = info[0], info[1], info[2]
     depth, row_count = same[0].shape[1], same[0].shape[2]
 
-    def copy(c, d, half, k):
+    def copy(c, d, half, k, m, n):
         start = pl.multiple_of(half * row_count, row_count)
         return pltpu.make_async_copy(
-            ready.at[k], out.at[c + first, d, :, pl.ds(start, row_count)], sent.at[k]
+            ready.at[k, m : m + n],
+            out.at[c + first, d, m : m + n, pl.ds(start, row_count)],
+            sent.at[k],
         )
 
     @pl.when((tile == 0) & (is_hub == 1))
@@ -100,28 +107,27 @@
 
     @pl.when(step >= SLOTS)
     def _():
-        copy(0, 0, 0, slot).wait()
+        copy(0, 0, 0, slot, 0, row_count).wait()
 
     def multiply(blocks):
-        right = jnp.concatenate([block[tile // 2] for block in blocks], axis=0)
+        right = jnp.concatenate([block[lax.rem(tile, 3)] for block in blocks], axis=0)
         for m in range(0, row_count, TILE):
             value = jnp.dot(turned[m : m + TILE, :], right, preferred_element_type=jnp.float32)
             ready[slot, m : m + TILE, :] = value * (1.0 / scale) if scale & (scale - 1) == 0 else value / scale
-
-    @pl.when(tile % 2 == 0)
+            copy(component, lax.rem(tile, 3), core ^ (tile // 3), slot, m, TILE).start()
+
+    @pl.when(tile < 3)
     def _():
         multiply(same)
 
-    @pl.when(tile % 2 == 1)
+    @pl.when(tile >= 3)
     def _():
         multiply(partner)
 
-    copy(component, tile // 2, core ^ (tile % 2), slot).start()
-
     @pl.when(step == 6 * components - 1)
     def _():
         for k in range(SLOTS):
-            copy(0, 0, 0, k).wait()
+            copy(0, 0, 0, k, 0, row_count).wait()
 
 
 def covariance_part(info, first, components, same, partner, rows, count_all, so_far):
@@ -148,7 +154,7 @@
         ],
         input_output_aliases=aliases,
         compiler_params=pltpu.CompilerParams(
-            dimension_semantics=("arbitrary", "arbitrary"), vmem_limit_bytes=48 * 2**20
+            dimension_semantics=("arbitrary", "arbitrary"), vmem_limit_bytes=24 * 2**20
         ),
         cost_estimate=pl.CostEstimate(
             flops=2 * count * depth * components * 6 * row_count * row_count,
@@ -172,7 +178,7 @@
     chip = jnp.concatenate([jnp.where(lower, deviation, other), jnp.where(lower, other, deviation)], axis=1)
     left, right = chip[:, :, :row_count], chip[:, :, row_count:]
     mine, theirs = jnp.where(lower, left, right), jnp.where(lower, right, left)
-    mine, theirs, mine_early, mine_late = lax.optimization_barrier((mine, theirs, mine[:2], mine[2:]))
+    mine, theirs, mine_early, mine_late = lax.optimization_barrier((mine, theirs, mine[:EARLY], mine[EARLY:]))
 
     def rows_of(block):
         return [
@@ -199,8 +205,8 @@
     late = rows_of(mine_late)
     partner = [theirs] + [lax.ppermute(same[s], "frames", swap) for s in every if s]
     info = jnp.stack([core, plane, (place // 2 == plane).astype(jnp.int32)]).astype(jnp.int32)
-    product = covariance_part(info, 0, 2, same, partner, early, count_all, None)
-    product = covariance_part(info, 2, 1, same, partner, late, count_all, product)
+    product = covariance_part(info, 0, EARLY, same, partner, early, count_all, None)
+    product = covariance_part(info, EARLY, 3 - EARLY, same, partner, late, count_all, product)
     return jnp.transpose(product, (0, 2, 1, 3))
 
 

time: 170 us -> 172 us (1.012)
  the two profiles are of different devices: /device:TPU:0 before, /device:TPU:26 now
where the time goes in v1:
time: 172 us; the launch traced here: 171 us
  waiting for transfers between devices  95.6 us (56%)
  starting transfers between devices  39.2 us (23%)
  Pallas kernels  20.6 us (12%)
  local copies, waits for them, and re-layouts  5.1 us (3%)
  matrix products  4.58 us (3%)
  other arithmetic  4.28 us (2%)
  between operations  1.9 us (1%)
    ppermute x8, waiting for transfers between devices, rows_of(): lax.ppermute(block, both, [(device(q ^ t ^ z, c, q), device(q, c, z)) for...  55.7 us
    ppermute x3, waiting for transfers between devices, direct(): lax.ppermute(mine, 'frames', [(2 * (q ^ s) + c, 2 * q + c) for q in every...  25.5 us
    pallas_call x2, Pallas kernels, covariance_part(): pl.pallas_call(functools.partial(product_kernel, count, count_all, compon...  20.6 us
    ppermute x8, starting transfers between devices, rows_of(): lax.ppermute(block, both, [(device(q ^ t ^ z, c, q), device(q, c, z)) for...  19.2 us
    ppermute x14, starting transfers between devices, sum_over(): lax.ppermute(value, axis, [(i, i ^ m) for i in range(size)])  16 us
    ppermute x14, waiting for transfers between devices, sum_over(): lax.ppermute(value, axis, [(i, i ^ m) for i in range(size)])  12.4 us
    dot_general x2, matrix products, superpose(): jnp.einsum('cfa,da->dcf', coords, weights, precision=highest)  3.91 us
    ppermute x3, starting transfers between devices, direct(): lax.ppermute(mine, 'frames', [(2 * (q ^ s) + c, 2 * q + c) for q in every...  3.49 us
  transfers between devices with their start and end apart: 29, of which 25 were waited for; matrix products, arithmetic and copies ran while one was open for 0% of the time, Pallas kernels for 4%

profile of v1, /device:TPU:26, one launch (start us, length us, event | category | flops | bytes accessed | tf_op | source)
XLA Modules:
  0.0 171.2 jit_solution(2712486097028901125)
XLA Ops:
  0.6 1.0 reduce_sum.49
  1.6 2.6 %fusion.2 = f32[4,3,64]{2,0,1:T(4,128)S(1)} fusion(f32[64,3,1536]{2,0,1:T(8,128)} %param.2, f32[3,1536]{1,0:T(4,128)} %param.3), kind=kOutput, calls=%fused_computation.7 | convolution fusion | flops 14155776 | bytes 1201152 | tf_op jit(solution)/shard_map/cfa,da->dcf/dot_general | solution.py:62
  4.4 0.2 collective-permute-start.2
  4.6 1.7 collective-permute-start.1
  6.3 2.5 %collective-permute-start = (f32[15,64]{1,0:T(8,128)S(1)}, f32[15,64]{1,0:T(8,128)S(1)}, u32[]{:S(2)}, u32[]{:S(2)}) collective-permute-start(f32[15,64]{1,0:T(8,128)S(1)} %pad_maximum_fusion.2), channel_id=1, source_target_pairs={{0,1},{1,0},{2,3},{3,2},{4,5},{5,4},{6,7},{7,6},{8,9},{9,8},{10,11... | collective-permute-start | bytes 11528 | tf_op jit(solution)/shard_map/ppermute | solution.py:46
  8.8 1.1 collective-permute-done.2
  9.9 0.6 collective-permute-done
  11.8 0.1 bitcast_subtract_fusion
  12.1 0.7 convolution_bitcast_fusion
  12.8 1.2 collective-permute-done.3
  14.0 1.6 collective-permute-start.6
  15.6 0.5 collective-permute-start.5
  16.1 1.5 collective-permute-start.4
  17.6 1.2 collective-permute-done.6
  18.8 0.6 collective-permute-done.5
  19.4 0.5 collective-permute-done.4
  20.1 1.3 fusion
  21.6 2.4 %collective-permute-start.9 = (f32[12,64]{1,0:T(8,128)S(1)}, f32[12,64]{1,0:T(8,128)S(1)}, u32[]{:S(2)}, u32[]{:S(2)}) collective-permute-start(f32[12,64]{1,0:T(8,128)S(1)} %pad_maximum_fusion.3), channel_id=1, source_target_pairs={{0,3},{1,2},{2,1},{3,0},{4,7},{5,6},{6,5},{7,4},{8,11},{9,10},{10,... | collective-permute-start | bytes 9224 | tf_op jit(solution)/shard_map/ppermute | solution.py:46
  23.9 1.1 collective-permute-start.8
  25.1 0.9 collective-permute-start.7
  26.0 1.1 collective-permute-done.9
  27.0 1.5 collective-permute-done.8
  28.5 0.2 collective-permute-done.7
  30.3 0.3 multiply_add_fusion.2
  30.7 1.2 collective-permute-done.10
  31.9 2.5 %collective-permute-start.13 = (f32[3,1536]{1,0:T(4,128)S(1)}, f32[3,1536]{1,0:T(4,128)S(1)}, u32[]{:S(2)}, u32[]{:S(2)}) collective-permute-start(f32[3,1536]{1,0:T(4,128)S(1)} %add.314), channel_id=1, source_target_pairs={{0,24},{4,28},{8,16},{12,20},{16,8},{20,12},{24,0},{28,4},{1,25},{... | collective-permute-start | bytes 55304 | tf_op jit(solution)/shard_map/ppermute | solution.py:46
  34.4 0.5 collective-permute-start.12
  34.9 0.5 collective-permute-start.11
  35.5 1.2 collective-permute-done.13
  36.7 1.5 collective-permute-done.12
  38.3 0.5 collective-permute-done.11
  39.0 2.0 %collective-permute-done.14 = bf16[3,64,1536]{2,1,0:T(8,128)(2,1)S(1)} collective-permute-done((bf16[3,64,1536]{2,1,0:T(8,128)(2,1)S(1)}, bf16[3,64,1536]{2,1,0:T(8,128)(2,1)S(1)}, u32[]{:S(2)}, u32[]{:S(2)}) %collective-permute-start.14) | collective-permute-done | bytes 589856 | tf_op jit(solution)/shard_map/ppermute | solution.py:176
  41.0 0.2 broadcast_select_fusion.1
  41.2 0.2 broadcast_select_fusion.2
  41.4 0.7 slice.829
  42.1 0.8 slice.830
  42.9 1.5 collective-permute-start.17
  44.4 0.5 collective-permute-start.16
  44.9 1.5 collective-permute-start.15
  46.4 13.7 %collective-permute-done.17.refs_3_ = bf16[3,128,768]{2,1,0:T(8,128)(2,1)S(1)} collective-permute-done((bf16[3,128,768]{2,1,0:T(8,128)(2,1)S(1)}, bf16[3,128,768]{2,1,0:T(8,128)(2,1)S(1)}, u32[]{:S(2)}, u32[]{:S(2)}) %collective-permute-start.17) | collective-permute-done | bytes 589856 | tf_op jit(solution)/shard_map/ppermute | solution.py:201
  60.0 11.8 %collective-permute-done.16.refs_2_ = bf16[3,128,768]{2,1,0:T(8,128)(2,1)S(1)} collective-permute-done((bf16[3,128,768]{2,1,0:T(8,128)(2,1)S(1)}, bf16[3,128,768]{2,1,0:T(8,128)(2,1)S(1)}, u32[]{:S(2)}, u32[]{:S(2)}) %collective-permute-start.16) | collective-permute-done | bytes 589856 | tf_op jit(solution)/shard_map/ppermute | solution.py:201
  71.9 0.4 collective-permute-start.18
  72.3 4.0 %collective-permute-start.28 = (bf16[1,128,768]{2,1,0:T(8,128)(2,1)}, bf16[1,128,768]{2,1,0:T(8,128)(2,1)S(1)}, u32[]{:S(2)}, u32[]{:S(2)}) collective-permute-start(bf16[1,128,768]{2,1,0:T(8,128)(2,1)} %slice.829), channel_id=1, source_target_pairs={{16,1},{8,2},{0,3},{20,5},{12,6},{4,7},{17,8},{1,10},{9,11},{21,12... | collective-permute-start | bytes 589832 | tf_op jit(solution)/shard_map/ppermute | solution.py:185
  76.3 1.9 %collective-permute-start.27 = (bf16[1,128,768]{2,1,0:T(8,128)(2,1)}, bf16[1,128,768]{2,1,0:T(8,128)(2,1)S(1)}, u32[]{:S(2)}, u32[]{:S(2)}) collective-permute-start(bf16[1,128,768]{2,1,0:T(8,128)(2,1)} %slice.829), channel_id=1, source_target_pairs={{24,1},{0,2},{8,3},{28,5},{4,6},{12,7},{25,8},{9,10},{1,11},{29,12... | collective-permute-start | bytes 589832 | tf_op jit(solution)/shard_map/ppermute | solution.py:185
  78.2 12.8 %collective-permute-done.28.refs_11_ = bf16[1,128,768]{2,1,0:T(8,128)(2,1)S(1)} collective-permute-done((bf16[1,128,768]{2,1,0:T(8,128)(2,1)}, bf16[1,128,768]{2,1,0:T(8,128)(2,1)S(1)}, u32[]{:S(2)}, u32[]{:S(2)}) %collective-permute-start.28) | collective-permute-done | bytes 196640 | tf_op jit(solution)/shard_map/ppermute | solution.py:185
  91.0 0.7 copy-done
  91.7 1.3 collective-permute-start.26
  93.0 3.5 %collective-permute-done.27.refs_10_ = bf16[1,128,768]{2,1,0:T(8,128)(2,1)S(1)} collective-permute-done((bf16[1,128,768]{2,1,0:T(8,128)(2,1)}, bf16[1,128,768]{2,1,0:T(8,128)(2,1)S(1)}, u32[]{:S(2)}, u32[]{:S(2)}) %collective-permute-start.27) | collective-permute-done | bytes 196640 | tf_op jit(solution)/shard_map/ppermute | solution.py:185
  96.5 0.7 copy-done.2
  97.2 5.0 %collective-permute-start.25 = (bf16[1,128,768]{2,1,0:T(8,128)(2,1)}, bf16[1,128,768]{2,1,0:T(8,128)(2,1)}, u32[]{:S(2)}, u32[]{:S(2)}) collective-permute-start(bf16[1,128,768]{2,1,0:T(8,128)(2,1)} %slice.829), channel_id=1, source_target_pairs={{8,1},{16,2},{24,3},{12,5},{20,6},{28,7},{9,8},{25,10},{17,11},{13... | collective-permute-start | bytes 589832 | tf_op jit(solution)/shard_map/ppermute | solution.py:185
  102.2 7.8 %collective-permute-done.26.refs_9_ = bf16[1,128,768]{2,1,0:T(8,128)(2,1)} collective-permute-done((bf16[1,128,768]{2,1,0:T(8,128)(2,1)}, bf16[1,128,768]{2,1,0:T(8,128)(2,1)}, u32[]{:S(2)}, u32[]{:S(2)}) %collective-permute-start.26) | collective-permute-done | bytes 196640 | tf_op jit(solution)/shard_map/ppermute | solution.py:185
  110.0 1.9 %collective-permute-start.24 = (bf16[2,128,768]{2,1,0:T(8,128)(2,1)}, bf16[2,128,768]{2,1,0:T(8,128)(2,1)S(1)}, u32[]{:S(2)}, u32[]{:S(2)}) collective-permute-start(bf16[2,128,768]{2,1,0:T(8,128)(2,1)} %slice.830), channel_id=1, source_target_pairs={{16,1},{8,2},{0,3},{20,5},{12,6},{4,7},{17,8},{1,10},{9,11},{21,12... | collective-permute-start | bytes 1179656 | tf_op jit(solution)/shard_map/ppermute | solution.py:185
  111.9 4.7 %collective-permute-done.25.refs_8_ = bf16[1,128,768]{2,1,0:T(8,128)(2,1)} collective-permute-done((bf16[1,128,768]{2,1,0:T(8,128)(2,1)}, bf16[1,128,768]{2,1,0:T(8,128)(2,1)}, u32[]{:S(2)}, u32[]{:S(2)}) %collective-permute-start.25) | collective-permute-done | bytes 196640 | tf_op jit(solution)/shard_map/ppermute | solution.py:185
  116.7 1.9 %collective-permute-start.23 = (bf16[2,128,768]{2,1,0:T(8,128)(2,1)}, bf16[2,128,768]{2,1,0:T(8,128)(2,1)S(1)}, u32[]{:S(2)}, u32[]{:S(2)}) collective-permute-start(bf16[2,128,768]{2,1,0:T(8,128)(2,1)} %slice.830), channel_id=1, source_target_pairs={{24,1},{0,2},{8,3},{28,5},{4,6},{12,7},{25,8},{9,10},{1,11},{29,12... | collective-permute-start | bytes 1179656 | tf_op jit(solution)/shard_map/ppermute | solution.py:185
  118.6 1.3 collective-permute-start.22
  119.9 1.9 %collective-permute-start.21 = (bf16[2,128,768]{2,1,0:T(8,128)(2,1)}, bf16[2,128,768]{2,1,0:T(8,128)(2,1)S(1)}, u32[]{:S(2)}, u32[]{:S(2)}) collective-permute-start(bf16[2,128,768]{2,1,0:T(8,128)(2,1)} %slice.830), channel_id=1, source_target_pairs={{8,1},{16,2},{24,3},{12,5},{20,6},{28,7},{9,8},{25,10},{17,11},{13... | collective-permute-start | bytes 1179656 | tf_op jit(solution)/shard_map/ppermute | solution.py:185
  121.9 0.9 copy-done.1
  122.8 0.9 copy-done.3
  123.8 7.7 %shard_map.41.refs_12_ = f32[3,3,768,1536]{3,2,1,0:T(8,128)} custom-call(s32[3]{0:T(128)S(1)} %pad_add_fusion.info, bf16[3,128,768]{2,1,0:T(8,128)(2,1)S(1)} %get-tuple-element.6.refs_0_, bf16[3,128,768]{2,1,0:T(8,128)(2,1)S(1)} %collective-permute-done.15.refs_1_, bf16[3,128,768]{2,1,0:T(8,128)(2,1)S(1)} %collective-permute-done.16.refs_2_, ...), custom_call_target="tpu_custom_call" | custom-call | flops 3623878656 | bytes 14155776 | tf_op jit(solution)/shard_map/pallas_call | solution.py:144
  131.4 0.1 collective-permute-done.24.refs_11_
  131.6 15.1 %collective-permute-done.23.refs_10_ = bf16[2,128,768]{2,1,0:T(8,128)(2,1)S(1)} collective-permute-done((bf16[2,128,768]{2,1,0:T(8,128)(2,1)}, bf16[2,128,768]{2,1,0:T(8,128)(2,1)S(1)}, u32[]{:S(2)}, u32[]{:S(2)}) %collective-permute-start.23) | collective-permute-done | bytes 393248 | tf_op jit(solution)/shard_map/ppermute | solution.py:185
  146.7 4.9 %collective-permute-done.22.refs_9_ = bf16[2,128,768]{2,1,0:T(8,128)(2,1)S(1)} collective-permute-done((bf16[2,128,768]{2,1,0:T(8,128)(2,1)}, bf16[2,128,768]{2,1,0:T(8,128)(2,1)S(1)}, u32[]{:S(2)}, u32[]{:S(2)}) %collective-permute-start.22) | collective-permute-done | bytes 393248 | tf_op jit(solution)/shard_map/ppermute | solution.py:185
  151.6 6.7 %collective-permute-done.21.refs_8_ = bf16[2,128,768]{2,1,0:T(8,128)(2,1)S(1)} collective-permute-done((bf16[2,128,768]{2,1,0:T(8,128)(2,1)}, bf16[2,128,768]{2,1,0:T(8,128)(2,1)S(1)}, u32[]{:S(2)}, u32[]{:S(2)}) %collective-permute-start.21) | collective-permute-done | bytes 393248 | tf_op jit(solution)/shard_map/ppermute | solution.py:185
  158.3 12.9 %shard_map.42 = f32[3,3,768,1536]{3,2,1,0:T(8,128)} custom-call(s32[3]{0:T(128)S(1)} %pad_add_fusion.info, bf16[3,128,768]{2,1,0:T(8,128)(2,1)S(1)} %get-tuple-element.6.refs_0_, bf16[3,128,768]{2,1,0:T(8,128)(2,1)S(1)} %collective-permute-done.15.refs_1_, bf16[3,128,768]{2,1,0:T(8,128)(2,1)S(1)} %collective-permute-done.16.refs_2_, ...), custom_call_target="tpu_custom_call", output_to_operand_aliasing={{}: (13, {})} | custom-call | flops 7247757312 | bytes 28311552 | tf_op jit(solution)/shard_map/pallas_call | solution.py:144
  (189 shorter events, 3.2 us)
Async XLA Ops:
  0.6 11.1 %copy-start.4 = (f32[64,3,1536]{2,0,1:T(8,128)S(1)}, f32[64,3,1536]{2,0,1:T(8,128)}, u32[]{:S(2)}) copy-start(f32[64,3,1536]{2,0,1:T(8,128)} %param.2) | copy-start | bytes 3538948
  4.4 5.4 %collective-permute-start.2 = (f32[15,64]{1,0:T(8,128)S(1)}, f32[15,64]{1,0:T(8,128)S(1)}, u32[]{:S(2)}, u32[]{:S(2)}) collective-permute-start(f32[15,64]{1,0:T(8,128)S(1)} %pad_maximum_fusion.2), channel_id=1, source_target_pairs={{0,3},{1,2},{2,1},{3,0},{4,7},{5,6},{6,5},{7,4},{8,11},{9,10},{10,... | collective-permute-start | bytes 11528 | tf_op jit(solution)/shard_map/ppermute | solution.py:46
  4.6 5.2 %collective-permute-start.1 = (f32[15,64]{1,0:T(8,128)S(1)}, f32[15,64]{1,0:T(8,128)S(1)}, u32[]{:S(2)}, u32[]{:S(2)}) collective-permute-start(f32[15,64]{1,0:T(8,128)S(1)} %pad_maximum_fusion.2), channel_id=1, source_target_pairs={{0,2},{1,3},{2,0},{3,1},{4,6},{5,7},{6,4},{7,5},{8,10},{9,11},{10,... | collective-permute-start | bytes 11528 | tf_op jit(solution)/shard_map/ppermute | solution.py:46
  6.3 4.1 %collective-permute-start = (f32[15,64]{1,0:T(8,128)S(1)}, f32[15,64]{1,0:T(8,128)S(1)}, u32[]{:S(2)}, u32[]{:S(2)}) collective-permute-start(f32[15,64]{1,0:T(8,128)S(1)} %pad_maximum_fusion.2), channel_id=1, source_target_pairs={{0,1},{1,0},{2,3},{3,2},{4,5},{5,4},{6,7},{7,6},{8,9},{9,8},{10,11... | collective-permute-start | bytes 11528 | tf_op jit(solution)/shard_map/ppermute | solution.py:46
  12.8 1.3 collective-permute-start.3
  14.0 4.8 %collective-permute-start.6 = (f32[3,1536]{1,0:T(4,128)S(1)}, f32[3,1536]{1,0:T(4,128)S(1)}, u32[]{:S(2)}, u32[]{:S(2)}) collective-permute-start(f32[3,1536]{1,0:T(4,128)S(1)} %add.277), channel_id=1, source_target_pairs={{0,24},{4,28},{8,16},{12,20},{16,8},{20,12},{24,0},{28,4},{1,25},{... | collective-permute-start | bytes 55304 | tf_op jit(solution)/shard_map/ppermute | solution.py:46
  15.6 3.8 %collective-permute-start.5 = (f32[3,1536]{1,0:T(4,128)S(1)}, f32[3,1536]{1,0:T(4,128)S(1)}, u32[]{:S(2)}, u32[]{:S(2)}) collective-permute-start(f32[3,1536]{1,0:T(4,128)S(1)} %add.277), channel_id=1, source_target_pairs={{0,16},{4,20},{8,24},{12,28},{16,0},{20,4},{24,8},{28,12},{1,17},{... | collective-permute-start | bytes 55304 | tf_op jit(solution)/shard_map/ppermute | solution.py:46
  16.1 3.8 %collective-permute-start.4 = (f32[3,1536]{1,0:T(4,128)S(1)}, f32[3,1536]{1,0:T(4,128)S(1)}, u32[]{:S(2)}, u32[]{:S(2)}) collective-permute-start(f32[3,1536]{1,0:T(4,128)S(1)} %add.277), channel_id=1, source_target_pairs={{0,8},{4,12},{8,0},{12,4},{16,24},{20,28},{24,16},{28,20},{1,9},{5... | collective-permute-start | bytes 55304 | tf_op jit(solution)/shard_map/ppermute | solution.py:46
  21.6 5.5 %collective-permute-start.9 = (f32[12,64]{1,0:T(8,128)S(1)}, f32[12,64]{1,0:T(8,128)S(1)}, u32[]{:S(2)}, u32[]{:S(2)}) collective-permute-start(f32[12,64]{1,0:T(8,128)S(1)} %pad_maximum_fusion.3), channel_id=1, source_target_pairs={{0,3},{1,2},{2,1},{3,0},{4,7},{5,6},{6,5},{7,4},{8,11},{9,10},{10,... | collective-permute-start | bytes 9224 | tf_op jit(solution)/shard_map/ppermute | solution.py:46
  23.9 4.5 %collective-permute-start.8 = (f32[12,64]{1,0:T(8,128)S(1)}, f32[12,64]{1,0:T(8,128)S(1)}, u32[]{:S(2)}, u32[]{:S(2)}) collective-permute-start(f32[12,64]{1,0:T(8,128)S(1)} %pad_maximum_fusion.3), channel_id=1, source_target_pairs={{0,2},{1,3},{2,0},{3,1},{4,6},{5,7},{6,4},{7,5},{8,10},{9,11},{10,... | collective-permute-start | bytes 9224 | tf_op jit(solution)/shard_map/ppermute | solution.py:46
  25.1 3.7 %collective-permute-start.7 = (f32[12,64]{1,0:T(8,128)S(1)}, f32[12,64]{1,0:T(8,128)S(1)}, u32[]{:S(2)}, u32[]{:S(2)}) collective-permute-start(f32[12,64]{1,0:T(8,128)S(1)} %pad_maximum_fusion.3), channel_id=1, source_target_pairs={{0,1},{1,0},{2,3},{3,2},{4,5},{5,4},{6,7},{7,6},{8,9},{9,8},{10,11... | collective-permute-start | bytes 9224 | tf_op jit(solution)/shard_map/ppermute | solution.py:46
  30.7 1.3 collective-permute-start.10
  31.9 4.8 %collective-permute-start.13 = (f32[3,1536]{1,0:T(4,128)S(1)}, f32[3,1536]{1,0:T(4,128)S(1)}, u32[]{:S(2)}, u32[]{:S(2)}) collective-permute-start(f32[3,1536]{1,0:T(4,128)S(1)} %add.314), channel_id=1, source_target_pairs={{0,24},{4,28},{8,16},{12,20},{16,8},{20,12},{24,0},{28,4},{1,25},{... | collective-permute-start | bytes 55304 | tf_op jit(solution)/shard_map/ppermute | solution.py:46
  34.4 3.8 %collective-permute-start.12 = (f32[3,1536]{1,0:T(4,128)S(1)}, f32[3,1536]{1,0:T(4,128)S(1)}, u32[]{:S(2)}, u32[]{:S(2)}) collective-permute-start(f32[3,1536]{1,0:T(4,128)S(1)} %add.314), channel_id=1, source_target_pairs={{0,16},{4,20},{8,24},{12,28},{16,0},{20,4},{24,8},{28,12},{1,17},{... | collective-permute-start | bytes 55304 | tf_op jit(solution)/shard_map/ppermute | solution.py:46
  34.9 3.8 %collective-permute-start.11 = (f32[3,1536]{1,0:T(4,128)S(1)}, f32[3,1536]{1,0:T(4,128)S(1)}, u32[]{:S(2)}, u32[]{:S(2)}) collective-permute-start(f32[3,1536]{1,0:T(4,128)S(1)} %add.314), channel_id=1, source_target_pairs={{0,8},{4,12},{8,0},{12,4},{16,24},{20,28},{24,16},{28,20},{1,9},{5... | collective-permute-start | bytes 55304 | tf_op jit(solution)/shard_map/ppermute | solution.py:46
  38.8 2.4 %copy-start.5 = (f32[3,1536]{1,0:T(4,128)}, f32[3,1536]{1,0:T(4,128)S(1)}, u32[]{:S(2)}) copy-start(f32[3,1536]{1,0:T(4,128)S(1)} %add_multiply_fusion) | copy-start | bytes 55300
  38.9 2.1 %collective-permute-start.14 = (bf16[3,64,1536]{2,1,0:T(8,128)(2,1)S(1)}, bf16[3,64,1536]{2,1,0:T(8,128)(2,1)S(1)}, u32[]{:S(2)}, u32[]{:S(2)}) collective-permute-start(bf16[3,64,1536]{2,1,0:T(8,128)(2,1)S(1)} %subtract_convert_fusion), channel_id=1, source_target_pairs={{0,4},{4,0},{8,12},{12,8},{16,20},{20,16},{24,28},{28,24},{1,5},{5... | collective-permute-start | bytes 1769480 | tf_op jit(solution)/shard_map/ppermute | solution.py:176
  42.9 17.1 %collective-permute-start.17 = (bf16[3,128,768]{2,1,0:T(8,128)(2,1)S(1)}, bf16[3,128,768]{2,1,0:T(8,128)(2,1)S(1)}, u32[]{:S(2)}, u32[]{:S(2)}) collective-permute-start(bf16[3,128,768]{2,1,0:T(8,128)(2,1)S(1)} %get-tuple-element.6.refs_0_), channel_id=1, source_target_pairs={{24,0},{28,4},{16,8},{20,12},{8,16},{12,20},{0,24},{4,28},{25,1},{... | collective-permute-start | bytes 1769480 | tf_op jit(solution)/shard_map/ppermute | solution.py:201
  44.4 27.4 %collective-permute-start.16 = (bf16[3,128,768]{2,1,0:T(8,128)(2,1)S(1)}, bf16[3,128,768]{2,1,0:T(8,128)(2,1)S(1)}, u32[]{:S(2)}, u32[]{:S(2)}) collective-permute-start(bf16[3,128,768]{2,1,0:T(8,128)(2,1)S(1)} %get-tuple-element.6.refs_0_), channel_id=1, source_target_pairs={{16,0},{20,4},{24,8},{28,12},{0,16},{4,20},{8,24},{12,28},{17,1},{... | collective-permute-start | bytes 1769480 | tf_op jit(solution)/shard_map/ppermute | solution.py:201
  44.9 27.0 %collective-permute-start.15 = (bf16[3,128,768]{2,1,0:T(8,128)(2,1)S(1)}, bf16[3,128,768]{2,1,0:T(8,128)(2,1)S(1)}, u32[]{:S(2)}, u32[]{:S(2)}) collective-permute-start(bf16[3,128,768]{2,1,0:T(8,128)(2,1)S(1)} %get-tuple-element.6.refs_0_), channel_id=1, source_target_pairs={{8,0},{12,4},{0,8},{4,12},{24,16},{28,20},{16,24},{20,28},{9,1},{1... | collective-permute-start | bytes 1769480 | tf_op jit(solution)/shard_map/ppermute | solution.py:201
  60.0 58.6 %collective-permute-start.20 = (bf16[3,128,768]{2,1,0:T(8,128)(2,1)S(1)}, bf16[3,128,768]{2,1,0:T(8,128)(2,1)S(1)}, u32[]{:S(2)}, u32[]{:S(2)}) collective-permute-start(bf16[3,128,768]{2,1,0:T(8,128)(2,1)S(1)} %collective-permute-done.17.refs_3_), channel_id=1, source_target_pairs={{0,4},{4,0},{8,12},{12,8},{16,20},{20,16},{24,28},{28,24},{1,5},{5... | collective-permute-start | bytes 1769480 | tf_op jit(solution)/shard_map/ppermute | solution.py:206
  71.8 48.1 %collective-permute-start.19 = (bf16[3,128,768]{2,1,0:T(8,128)(2,1)S(1)}, bf16[3,128,768]{2,1,0:T(8,128)(2,1)}, u32[]{:S(2)}, u32[]{:S(2)}) collective-permute-start(bf16[3,128,768]{2,1,0:T(8,128)(2,1)S(1)} %collective-permute-done.16.refs_2_), channel_id=1, source_target_pairs={{0,4},{4,0},{8,12},{12,8},{16,20},{20,16},{24,28},{28,24},{1,5},{5... | collective-permute-start | bytes 1769480 | tf_op jit(solution)/shard_map/ppermute | solution.py:206
  71.9 50.0 %collective-permute-start.18 = (bf16[3,128,768]{2,1,0:T(8,128)(2,1)S(1)}, bf16[3,128,768]{2,1,0:T(8,128)(2,1)}, u32[]{:S(2)}, u32[]{:S(2)}) collective-permute-start(bf16[3,128,768]{2,1,0:T(8,128)(2,1)S(1)} %collective-permute-done.15.refs_1_), channel_id=1, source_target_pairs={{0,4},{4,0},{8,12},{12,8},{16,20},{20,16},{24,28},{28,24},{1,5},{5... | collective-permute-start | bytes 1769480 | tf_op jit(solution)/shard_map/ppermute | solution.py:206
  72.3 18.7 %collective-permute-start.28 = (bf16[1,128,768]{2,1,0:T(8,128)(2,1)}, bf16[1,128,768]{2,1,0:T(8,128)(2,1)S(1)}, u32[]{:S(2)}, u32[]{:S(2)}) collective-permute-start(bf16[1,128,768]{2,1,0:T(8,128)(2,1)} %slice.829), channel_id=1, source_target_pairs={{16,1},{8,2},{0,3},{20,5},{12,6},{4,7},{17,8},{1,10},{9,11},{21,12... | collective-permute-start | bytes 589832 | tf_op jit(solution)/shard_map/ppermute | solution.py:185
  76.3 20.2 %collective-permute-start.27 = (bf16[1,128,768]{2,1,0:T(8,128)(2,1)}, bf16[1,128,768]{2,1,0:T(8,128)(2,1)S(1)}, u32[]{:S(2)}, u32[]{:S(2)}) collective-permute-start(bf16[1,128,768]{2,1,0:T(8,128)(2,1)} %slice.829), channel_id=1, source_target_pairs={{24,1},{0,2},{8,3},{28,5},{4,6},{12,7},{25,8},{9,10},{1,11},{29,12... | collective-permute-start | bytes 589832 | tf_op jit(solution)/shard_map/ppermute | solution.py:185
  91.0 0.7 copy-start
  91.7 18.3 %collective-permute-start.26 = (bf16[1,128,768]{2,1,0:T(8,128)(2,1)}, bf16[1,128,768]{2,1,0:T(8,128)(2,1)}, u32[]{:S(2)}, u32[]{:S(2)}) collective-permute-start(bf16[1,128,768]{2,1,0:T(8,128)(2,1)} %slice.829), channel_id=1, source_target_pairs={{0,1},{24,2},{16,3},{4,5},{28,6},{20,7},{1,8},{17,10},{25,11},{5,1... | collective-permute-start | bytes 589832 | tf_op jit(solution)/shard_map/ppermute | solution.py:185
  96.5 0.7 copy-start.2
  97.2 19.5 %collective-permute-start.25 = (bf16[1,128,768]{2,1,0:T(8,128)(2,1)}, bf16[1,128,768]{2,1,0:T(8,128)(2,1)}, u32[]{:S(2)}, u32[]{:S(2)}) collective-permute-start(bf16[1,128,768]{2,1,0:T(8,128)(2,1)} %slice.829), channel_id=1, source_target_pairs={{8,1},{16,2},{24,3},{12,5},{20,6},{28,7},{9,8},{25,10},{17,11},{13... | collective-permute-start | bytes 589832 | tf_op jit(solution)/shard_map/ppermute | solution.py:185
  110.0 21.6 %collective-permute-start.24 = (bf16[2,128,768]{2,1,0:T(8,128)(2,1)}, bf16[2,128,768]{2,1,0:T(8,128)(2,1)S(1)}, u32[]{:S(2)}, u32[]{:S(2)}) collective-permute-start(bf16[2,128,768]{2,1,0:T(8,128)(2,1)} %slice.830), channel_id=1, source_target_pairs={{16,1},{8,2},{0,3},{20,5},{12,6},{4,7},{17,8},{1,10},{9,11},{21,12... | collective-permute-start | bytes 1179656 | tf_op jit(solution)/shard_map/ppermute | solution.py:185
  116.7 30.0 %collective-permute-start.23 = (bf16[2,128,768]{2,1,0:T(8,128)(2,1)}, bf16[2,128,768]{2,1,0:T(8,128)(2,1)S(1)}, u32[]{:S(2)}, u32[]{:S(2)}) collective-permute-start(bf16[2,128,768]{2,1,0:T(8,128)(2,1)} %slice.830), channel_id=1, source_target_pairs={{24,1},{0,2},{8,3},{28,5},{4,6},{12,7},{25,8},{9,10},{1,11},{29,12... | collective-permute-start | bytes 1179656 | tf_op jit(solution)/shard_map/ppermute | solution.py:185
  118.6 33.0 %collective-permute-start.22 = (bf16[2,128,768]{2,1,0:T(8,128)(2,1)}, bf16[2,128,768]{2,1,0:T(8,128)(2,1)S(1)}, u32[]{:S(2)}, u32[]{:S(2)}) collective-permute-start(bf16[2,128,768]{2,1,0:T(8,128)(2,1)} %slice.830), channel_id=1, source_target_pairs={{0,1},{24,2},{16,3},{4,5},{28,6},{20,7},{1,8},{17,10},{25,11},{5,1... | collective-permute-start | bytes 1179656 | tf_op jit(solution)/shard_map/ppermute | solution.py:185
  119.9 38.4 %collective-permute-start.21 = (bf16[2,128,768]{2,1,0:T(8,128)(2,1)}, bf16[2,128,768]{2,1,0:T(8,128)(2,1)S(1)}, u32[]{:S(2)}, u32[]{:S(2)}) collective-permute-start(bf16[2,128,768]{2,1,0:T(8,128)(2,1)} %slice.830), channel_id=1, source_target_pairs={{8,1},{16,2},{24,3},{12,5},{20,6},{28,7},{9,8},{25,10},{17,11},{13... | collective-permute-start | bytes 1179656 | tf_op jit(solution)/shard_map/ppermute | solution.py:185
  121.9 0.9 copy-start.1
  122.8 0.9 copy-start.3

commit v2 on v1

--- a/solution.py
+++ b/solution.py
@@ -102,7 +102,7 @@
     @pl.when((tile == 0) & (is_hub == 0))
     def _():
         for t in range(count):
-            start = pl.multiple_of((plane ^ t) * depth, depth)
+            start = pl.multiple_of((plane ^ t ^ (core * (count - 1))) * depth, depth)
             turned[:, pl.ds(start, depth)] = row_blocks[t][component].T
 
     @pl.when(step >= SLOTS)
@@ -178,7 +178,8 @@
     chip = jnp.concatenate([jnp.where(lower, deviation, other), jnp.where(lower, other, deviation)], axis=1)
     left, right = chip[:, :, :row_count], chip[:, :, row_count:]
     mine, theirs = jnp.where(lower, left, right), jnp.where(lower, right, left)
-    mine, theirs, mine_early, mine_late = lax.optimization_barrier((mine, theirs, mine[:EARLY], mine[EARLY:]))
+    mine, theirs = lax.optimization_barrier((mine, theirs))
+    mine_early, mine_late = mine[:EARLY], mine[EARLY:]
 
     def rows_of(block):
         return [
@@ -186,7 +187,7 @@
                 block,
                 both,
                 [
-                    (device(q ^ t ^ z, c, q), device(q, c, z))
+                    (device(q ^ t ^ z ^ (planes - 1) * c, c, q), device(q, c, z))
                     for q in every
                     for c in range(2)
                     for z in every

time: 172 us -> 156 us (0.907)
  waiting for transfers between devices: 95.6 us -> 75.2 us
  starting transfers between devices: 39.2 us -> 44.9 us
    ppermute x8, waiting for transfers between devices: 55.7 us -> 35.3 us  [rows_of(): lax.ppermute(block, both, [(device(q ^ t ^ z ^ (planes - 1) * c, c, q), d...]
    ppermute x8, starting transfers between devices: 19.2 us -> 24.9 us  [rows_of(): lax.ppermute(block, both, [(device(q ^ t ^ z ^ (planes - 1) * c, c, q), d...]
  transfers between devices with their start and end apart: 29 -> 29, of which waited for: 25 -> 23; matrix products, arithmetic and copies ran while one was open for 0% -> 1% of each run, Pallas kernels for 4% -> 5%
where the time goes in v2:
time: 156 us
  waiting for transfers between devices  75.2 us (48%)
  starting transfers between devices  44.9 us (29%)
  Pallas kernels  20.6 us (13%)
  matrix products  4.58 us (3%)
  local copies, waits for them, and re-layouts  4.34 us (3%)
  other arithmetic  4.28 us (3%)
  between operations  2.08 us (1%)
    ppermute x8, waiting for transfers between devices, rows_of(): lax.ppermute(block, both, [(device(q ^ t ^ z ^ (planes - 1) * c, c, q), d...  35.3 us
    ppermute x3, waiting for transfers between devices, direct(): lax.ppermute(mine, 'frames', [(2 * (q ^ s) + c, 2 * q + c) for q in every...  25.5 us
    ppermute x8, starting transfers between devices, rows_of(): lax.ppermute(block, both, [(device(q ^ t ^ z ^ (planes - 1) * c, c, q), d...  24.9 us
    pallas_call x2, Pallas kernels, covariance_part(): pl.pallas_call(functools.partial(product_kernel, count, count_all, compon...  20.6 us
    ppermute x14, starting transfers between devices, sum_over(): lax.ppermute(value, axis, [(i, i ^ m) for i in range(size)])  16 us
    ppermute x14, waiting for transfers between devices, sum_over(): lax.ppermute(value, axis, [(i, i ^ m) for i in range(size)])  12.4 us
    dot_general x2, matrix products, superpose(): jnp.einsum('cfa,da->dcf', coords, weights, precision=highest)  3.9 us
    ppermute x3, starting transfers between devices, direct(): lax.ppermute(mine, 'frames', [(2 * (q ^ s) + c, 2 * q + c) for q in every...  3.55 us
  transfers between devices with their start and end apart: 29, of which 23 were waited for; matrix products, arithmetic and copies ran while one was open for 1% of the time, Pallas kernels for 5%

profile of v2, /device:TPU:26, one launch (start us, length us, event | category | flops | bytes accessed | tf_op | source)
XLA Modules:
  0.0 156.0 jit_solution(4791344063897194148)
XLA Ops:
  0.6 1.0 reduce_sum.49
  1.6 2.6 %fusion.2 = f32[4,3,64]{2,0,1:T(4,128)S(1)} fusion(f32[64,3,1536]{2,0,1:T(8,128)} %param.2, f32[3,1536]{1,0:T(4,128)} %param.3), kind=kOutput, calls=%fused_computation.7 | convolution fusion | flops 14155776 | bytes 1201152 | tf_op jit(solution)/shard_map/cfa,da->dcf/dot_general | solution.py:62
  4.4 0.2 collective-permute-start.2
  4.6 1.7 %collective-permute-start.1 = (f32[15,64]{1,0:T(8,128)S(1)}, f32[15,64]{1,0:T(8,128)S(1)}, u32[]{:S(2)}, u32[]{:S(2)}) collective-permute-start(f32[15,64]{1,0:T(8,128)S(1)} %pad_maximum_fusion.2), channel_id=1, source_target_pairs={{0,2},{1,3},{2,0},{3,1},{4,6},{5,7},{6,4},{7,5},{8,10},{9,11},{10,... | collective-permute-start | bytes 11528 | tf_op jit(solution)/shard_map/ppermute | solution.py:46
  6.3 2.5 %collective-permute-start = (f32[15,64]{1,0:T(8,128)S(1)}, f32[15,64]{1,0:T(8,128)S(1)}, u32[]{:S(2)}, u32[]{:S(2)}) collective-permute-start(f32[15,64]{1,0:T(8,128)S(1)} %pad_maximum_fusion.2), channel_id=1, source_target_pairs={{0,1},{1,0},{2,3},{3,2},{4,5},{5,4},{6,7},{7,6},{8,9},{9,8},{10,11... | collective-permute-start | bytes 11528 | tf_op jit(solution)/shard_map/ppermute | solution.py:46
  8.8 1.1 collective-permute-done.2
  9.9 0.6 collective-permute-done
  11.8 0.1 bitcast_subtract_fusion
  12.1 0.7 convolution_bitcast_fusion
  12.8 1.2 collective-permute-done.3
  14.0 1.6 collective-permute-start.6
  15.6 0.5 collective-permute-start.5
  16.1 1.5 collective-permute-start.4
  17.6 1.2 collective-permute-done.6
  18.8 0.6 collective-permute-done.5
  19.4 0.5 collective-permute-done.4
  19.9 0.1 fusion.29
  20.1 1.3 fusion
  21.6 2.4 %collective-permute-start.9 = (f32[12,64]{1,0:T(8,128)S(1)}, f32[12,64]{1,0:T(8,128)S(1)}, u32[]{:S(2)}, u32[]{:S(2)}) collective-permute-start(f32[12,64]{1,0:T(8,128)S(1)} %pad_maximum_fusion.3), channel_id=1, source_target_pairs={{0,3},{1,2},{2,1},{3,0},{4,7},{5,6},{6,5},{7,4},{8,11},{9,10},{10,... | collective-permute-start | bytes 9224 | tf_op jit(solution)/shard_map/ppermute | solution.py:46
  23.9 1.1 collective-permute-start.8
  25.1 0.9 collective-permute-start.7
  26.0 1.1 collective-permute-done.9
  27.0 1.5 collective-permute-done.8
  28.5 0.2 collective-permute-done.7
  30.3 0.3 multiply_add_fusion.2
  30.5 0.1 fusion.4
  30.7 1.2 collective-permute-done.10
  31.9 2.5 %collective-permute-start.13 = (f32[3,1536]{1,0:T(4,128)S(1)}, f32[3,1536]{1,0:T(4,128)S(1)}, u32[]{:S(2)}, u32[]{:S(2)}) collective-permute-start(f32[3,1536]{1,0:T(4,128)S(1)} %add.314), channel_id=1, source_target_pairs={{0,24},{4,28},{8,16},{12,20},{16,8},{20,12},{24,0},{28,4},{1,25},{... | collective-permute-start | bytes 55304 | tf_op jit(solution)/shard_map/ppermute | solution.py:46
  34.4 0.5 collective-permute-start.12
  34.9 0.5 collective-permute-start.11
  35.5 1.2 collective-permute-done.13
  36.7 1.5 collective-permute-done.12
  38.3 0.5 collective-permute-done.11
  38.8 0.1 subtract_convert_fusion
  39.0 2.0 %collective-permute-done.14 = bf16[3,64,1536]{2,1,0:T(8,128)(2,1)S(1)} collective-permute-done((bf16[3,64,1536]{2,1,0:T(8,128)(2,1)S(1)}, bf16[3,64,1536]{2,1,0:T(8,128)(2,1)S(1)}, u32[]{:S(2)}, u32[]{:S(2)}) %collective-permute-start.14) | collective-permute-done | bytes 589856 | tf_op jit(solution)/shard_map/ppermute | solution.py:176
  41.0 0.2 broadcast_select_fusion.1
  41.2 0.2 broadcast_select_fusion.2
  41.4 1.6 collective-permute-start.17
  43.0 0.5 collective-permute-start.16
  43.5 1.5 collective-permute-start.15
  45.0 13.7 %collective-permute-done.17.refs_3_ = bf16[3,128,768]{2,1,0:T(8,128)(2,1)S(1)} collective-permute-done((bf16[3,128,768]{2,1,0:T(8,128)(2,1)S(1)}, bf16[3,128,768]{2,1,0:T(8,128)(2,1)S(1)}, u32[]{:S(2)}, u32[]{:S(2)}) %collective-permute-start.17) | collective-permute-done | bytes 589856 | tf_op jit(solution)/shard_map/ppermute | solution.py:202
  58.6 11.8 %collective-permute-done.16.refs_2_ = bf16[3,128,768]{2,1,0:T(8,128)(2,1)S(1)} collective-permute-done((bf16[3,128,768]{2,1,0:T(8,128)(2,1)S(1)}, bf16[3,128,768]{2,1,0:T(8,128)(2,1)S(1)}, u32[]{:S(2)}, u32[]{:S(2)}) %collective-permute-start.16) | collective-permute-done | bytes 589856 | tf_op jit(solution)/shard_map/ppermute | solution.py:202
  70.5 0.4 collective-permute-start.18
  70.9 0.7 slice.665
  71.6 4.0 %collective-permute-start.28 = (bf16[1,128,768]{2,1,0:T(8,128)(2,1)}, bf16[1,128,768]{2,1,0:T(8,128)(2,1)S(1)}, u32[]{:S(2)}, u32[]{:S(2)}) collective-permute-start(bf16[1,128,768]{2,1,0:T(8,128)(2,1)} %slice.665), channel_id=1, source_target_pairs={{16,1},{8,2},{0,3},{12,5},{20,6},{28,7},{17,8},{1,10},{9,11},{13,1... | collective-permute-start | bytes 589832 | tf_op jit(solution)/shard_map/ppermute | solution.py:186
  75.5 1.9 %collective-permute-start.27 = (bf16[1,128,768]{2,1,0:T(8,128)(2,1)}, bf16[1,128,768]{2,1,0:T(8,128)(2,1)S(1)}, u32[]{:S(2)}, u32[]{:S(2)}) collective-permute-start(bf16[1,128,768]{2,1,0:T(8,128)(2,1)} %slice.665), channel_id=1, source_target_pairs={{24,1},{0,2},{8,3},{4,5},{28,6},{20,7},{25,8},{9,10},{1,11},{5,12}... | collective-permute-start | bytes 589832 | tf_op jit(solution)/shard_map/ppermute | solution.py:186
  77.5 4.9 %collective-permute-done.28.refs_11_ = bf16[1,128,768]{2,1,0:T(8,128)(2,1)S(1)} collective-permute-done((bf16[1,128,768]{2,1,0:T(8,128)(2,1)}, bf16[1,128,768]{2,1,0:T(8,128)(2,1)S(1)}, u32[]{:S(2)}, u32[]{:S(2)}) %collective-permute-start.28) | collective-permute-done | bytes 196640 | tf_op jit(solution)/shard_map/ppermute | solution.py:186
  82.4 0.7 copy-done
  83.0 1.3 collective-permute-start.26
  84.3 3.0 %collective-permute-done.27.refs_10_ = bf16[1,128,768]{2,1,0:T(8,128)(2,1)S(1)} collective-permute-done((bf16[1,128,768]{2,1,0:T(8,128)(2,1)}, bf16[1,128,768]{2,1,0:T(8,128)(2,1)S(1)}, u32[]{:S(2)}, u32[]{:S(2)}) %collective-permute-start.27) | collective-permute-done | bytes 196640 | tf_op jit(solution)/shard_map/ppermute | solution.py:186
  87.3 0.7 copy-done.2
  88.0 7.1 %collective-permute-start.25 = (bf16[1,128,768]{2,1,0:T(8,128)(2,1)}, bf16[1,128,768]{2,1,0:T(8,128)(2,1)}, u32[]{:S(2)}, u32[]{:S(2)}) collective-permute-start(bf16[1,128,768]{2,1,0:T(8,128)(2,1)} %slice.665), channel_id=1, source_target_pairs={{8,1},{16,2},{24,3},{20,5},{12,6},{4,7},{9,8},{25,10},{17,11},{21,... | collective-permute-start | bytes 589832 | tf_op jit(solution)/shard_map/ppermute | solution.py:186
  95.1 1.9 %collective-permute-start.24 = (bf16[2,128,768]{2,1,0:T(8,128)(2,1)S(1)}, bf16[2,128,768]{2,1,0:T(8,128)(2,1)S(1)}, u32[]{:S(2)}, u32[]{:S(2)}) collective-permute-start(bf16[2,128,768]{2,1,0:T(8,128)(2,1)S(1)} %slice.664), channel_id=1, source_target_pairs={{16,1},{8,2},{0,3},{12,5},{20,6},{28,7},{17,8},{1,10},{9,11},{13,1... | collective-permute-start | bytes 1179656 | tf_op jit(solution)/shard_map/ppermute | solution.py:186
  97.1 13.3 %collective-permute-done.25.refs_8_ = bf16[1,128,768]{2,1,0:T(8,128)(2,1)} collective-permute-done((bf16[1,128,768]{2,1,0:T(8,128)(2,1)}, bf16[1,128,768]{2,1,0:T(8,128)(2,1)}, u32[]{:S(2)}, u32[]{:S(2)}) %collective-permute-start.25) | collective-permute-done | bytes 196640 | tf_op jit(solution)/shard_map/ppermute | solution.py:186
  110.4 1.9 %collective-permute-start.23 = (bf16[2,128,768]{2,1,0:T(8,128)(2,1)S(1)}, bf16[2,128,768]{2,1,0:T(8,128)(2,1)S(1)}, u32[]{:S(2)}, u32[]{:S(2)}) collective-permute-start(bf16[2,128,768]{2,1,0:T(8,128)(2,1)S(1)} %slice.664), channel_id=1, source_target_pairs={{24,1},{0,2},{8,3},{4,5},{28,6},{20,7},{25,8},{9,10},{1,11},{5,12}... | collective-permute-start | bytes 1179656 | tf_op jit(solution)/shard_map/ppermute | solution.py:186
  112.3 1.3 collective-permute-start.22
  113.6 5.5 %collective-permute-start.21 = (bf16[2,128,768]{2,1,0:T(8,128)(2,1)S(1)}, bf16[2,128,768]{2,1,0:T(8,128)(2,1)S(1)}, u32[]{:S(2)}, u32[]{:S(2)}) collective-permute-start(bf16[2,128,768]{2,1,0:T(8,128)(2,1)S(1)} %slice.664), channel_id=1, source_target_pairs={{8,1},{16,2},{24,3},{20,5},{12,6},{4,7},{9,8},{25,10},{17,11},{21,... | collective-permute-start | bytes 1179656 | tf_op jit(solution)/shard_map/ppermute | solution.py:186
  119.2 0.9 copy-done.1
  120.1 0.9 copy-done.3
  121.1 7.7 %shard_map.41.refs_12_ = f32[3,3,768,1536]{3,2,1,0:T(8,128)} custom-call(s32[3]{0:T(128)S(1)} %pad_add_fusion.info, bf16[3,128,768]{2,1,0:T(8,128)(2,1)S(1)} %get-tuple-element.4.refs_0_, bf16[3,128,768]{2,1,0:T(8,128)(2,1)S(1)} %collective-permute-done.15.refs_1_, bf16[3,128,768]{2,1,0:T(8,128)(2,1)S(1)} %collective-permute-done.16.refs_2_, ...), custom_call_target="tpu_custom_call" | custom-call | flops 3623878656 | bytes 14155776 | tf_op jit(solution)/shard_map/pallas_call | solution.py:144
  128.7 4.8 %collective-permute-done.23.refs_10_ = bf16[2,128,768]{2,1,0:T(8,128)(2,1)S(1)} collective-permute-done((bf16[2,128,768]{2,1,0:T(8,128)(2,1)S(1)}, bf16[2,128,768]{2,1,0:T(8,128)(2,1)S(1)}, u32[]{:S(2)}, u32[]{:S(2)}) %collective-permute-start.23) | collective-permute-done | bytes 393248 | tf_op jit(solution)/shard_map/ppermute | solution.py:186
  133.5 0.2 collective-permute-done.22.refs_9_
  133.7 9.2 %collective-permute-done.21.refs_8_ = bf16[2,128,768]{2,1,0:T(8,128)(2,1)S(1)} collective-permute-done((bf16[2,128,768]{2,1,0:T(8,128)(2,1)S(1)}, bf16[2,128,768]{2,1,0:T(8,128)(2,1)S(1)}, u32[]{:S(2)}, u32[]{:S(2)}) %collective-permute-start.21) | collective-permute-done | bytes 393248 | tf_op jit(solution)/shard_map/ppermute | solution.py:186
  142.9 12.9 %shard_map.42 = f32[3,3,768,1536]{3,2,1,0:T(8,128)} custom-call(s32[3]{0:T(128)S(1)} %pad_add_fusion.info, bf16[3,128,768]{2,1,0:T(8,128)(2,1)S(1)} %get-tuple-element.4.refs_0_, bf16[3,128,768]{2,1,0:T(8,128)(2,1)S(1)} %collective-permute-done.15.refs_1_, bf16[3,128,768]{2,1,0:T(8,128)(2,1)S(1)} %collective-permute-done.16.refs_2_, ...), custom_call_target="tpu_custom_call", output_to_operand_aliasing={{}: (13, {})} | custom-call | flops 7247757312 | bytes 28311552 | tf_op jit(solution)/shard_map/pallas_call | solution.py:144
  (189 shorter events, 2.9 us)
Async XLA Ops:
  0.6 11.1 %copy-start.4 = (f32[64,3,1536]{2,0,1:T(8,128)S(1)}, f32[64,3,1536]{2,0,1:T(8,128)}, u32[]{:S(2)}) copy-start(f32[64,3,1536]{2,0,1:T(8,128)} %param.2) | copy-start | bytes 3538948
  4.4 5.4 %collective-permute-start.2 = (f32[15,64]{1,0:T(8,128)S(1)}, f32[15,64]{1,0:T(8,128)S(1)}, u32[]{:S(2)}, u32[]{:S(2)}) collective-permute-start(f32[15,64]{1,0:T(8,128)S(1)} %pad_maximum_fusion.2), channel_id=1, source_target_pairs={{0,3},{1,2},{2,1},{3,0},{4,7},{5,6},{6,5},{7,4},{8,11},{9,10},{10,... | collective-permute-start | bytes 11528 | tf_op jit(solution)/shard_map/ppermute | solution.py:46
  4.6 5.2 %collective-permute-start.1 = (f32[15,64]{1,0:T(8,128)S(1)}, f32[15,64]{1,0:T(8,128)S(1)}, u32[]{:S(2)}, u32[]{:S(2)}) collective-permute-start(f32[15,64]{1,0:T(8,128)S(1)} %pad_maximum_fusion.2), channel_id=1, source_target_pairs={{0,2},{1,3},{2,0},{3,1},{4,6},{5,7},{6,4},{7,5},{8,10},{9,11},{10,... | collective-permute-start | bytes 11528 | tf_op jit(solution)/shard_map/ppermute | solution.py:46
  6.3 4.1 %collective-permute-start = (f32[15,64]{1,0:T(8,128)S(1)}, f32[15,64]{1,0:T(8,128)S(1)}, u32[]{:S(2)}, u32[]{:S(2)}) collective-permute-start(f32[15,64]{1,0:T(8,128)S(1)} %pad_maximum_fusion.2), channel_id=1, source_target_pairs={{0,1},{1,0},{2,3},{3,2},{4,5},{5,4},{6,7},{7,6},{8,9},{9,8},{10,11... | collective-permute-start | bytes 11528 | tf_op jit(solution)/shard_map/ppermute | solution.py:46
  12.8 1.3 collective-permute-start.3
  14.0 4.8 %collective-permute-start.6 = (f32[3,1536]{1,0:T(4,128)S(1)}, f32[3,1536]{1,0:T(4,128)S(1)}, u32[]{:S(2)}, u32[]{:S(2)}) collective-permute-start(f32[3,1536]{1,0:T(4,128)S(1)} %add.277), channel_id=1, source_target_pairs={{0,24},{4,28},{8,16},{12,20},{16,8},{20,12},{24,0},{28,4},{1,25},{... | collective-permute-start | bytes 55304 | tf_op jit(solution)/shard_map/ppermute | solution.py:46
  15.6 3.8 %collective-permute-start.5 = (f32[3,1536]{1,0:T(4,128)S(1)}, f32[3,1536]{1,0:T(4,128)S(1)}, u32[]{:S(2)}, u32[]{:S(2)}) collective-permute-start(f32[3,1536]{1,0:T(4,128)S(1)} %add.277), channel_id=1, source_target_pairs={{0,16},{4,20},{8,24},{12,28},{16,0},{20,4},{24,8},{28,12},{1,17},{... | collective-permute-start | bytes 55304 | tf_op jit(solution)/shard_map/ppermute | solution.py:46
  16.1 3.8 %collective-permute-start.4 = (f32[3,1536]{1,0:T(4,128)S(1)}, f32[3,1536]{1,0:T(4,128)S(1)}, u32[]{:S(2)}, u32[]{:S(2)}) collective-permute-start(f32[3,1536]{1,0:T(4,128)S(1)} %add.277), channel_id=1, source_target_pairs={{0,8},{4,12},{8,0},{12,4},{16,24},{20,28},{24,16},{28,20},{1,9},{5... | collective-permute-start | bytes 55304 | tf_op jit(solution)/shard_map/ppermute | solution.py:46
  21.6 5.5 %collective-permute-start.9 = (f32[12,64]{1,0:T(8,128)S(1)}, f32[12,64]{1,0:T(8,128)S(1)}, u32[]{:S(2)}, u32[]{:S(2)}) collective-permute-start(f32[12,64]{1,0:T(8,128)S(1)} %pad_maximum_fusion.3), channel_id=1, source_target_pairs={{0,3},{1,2},{2,1},{3,0},{4,7},{5,6},{6,5},{7,4},{8,11},{9,10},{10,... | collective-permute-start | bytes 9224 | tf_op jit(solution)/shard_map/ppermute | solution.py:46
  23.9 4.5 %collective-permute-start.8 = (f32[12,64]{1,0:T(8,128)S(1)}, f32[12,64]{1,0:T(8,128)S(1)}, u32[]{:S(2)}, u32[]{:S(2)}) collective-permute-start(f32[12,64]{1,0:T(8,128)S(1)} %pad_maximum_fusion.3), channel_id=1, source_target_pairs={{0,2},{1,3},{2,0},{3,1},{4,6},{5,7},{6,4},{7,5},{8,10},{9,11},{10,... | collective-permute-start | bytes 9224 | tf_op jit(solution)/shard_map/ppermute | solution.py:46
  25.1 3.7 %collective-permute-start.7 = (f32[12,64]{1,0:T(8,128)S(1)}, f32[12,64]{1,0:T(8,128)S(1)}, u32[]{:S(2)}, u32[]{:S(2)}) collective-permute-start(f32[12,64]{1,0:T(8,128)S(1)} %pad_maximum_fusion.3), channel_id=1, source_target_pairs={{0,1},{1,0},{2,3},{3,2},{4,5},{5,4},{6,7},{7,6},{8,9},{9,8},{10,11... | collective-permute-start | bytes 9224 | tf_op jit(solution)/shard_map/ppermute | solution.py:46
  30.6 1.3 collective-permute-start.10
  31.9 4.8 %collective-permute-start.13 = (f32[3,1536]{1,0:T(4,128)S(1)}, f32[3,1536]{1,0:T(4,128)S(1)}, u32[]{:S(2)}, u32[]{:S(2)}) collective-permute-start(f32[3,1536]{1,0:T(4,128)S(1)} %add.314), channel_id=1, source_target_pairs={{0,24},{4,28},{8,16},{12,20},{16,8},{20,12},{24,0},{28,4},{1,25},{... | collective-permute-start | bytes 55304 | tf_op jit(solution)/shard_map/ppermute | solution.py:46
  34.4 3.8 %collective-permute-start.12 = (f32[3,1536]{1,0:T(4,128)S(1)}, f32[3,1536]{1,0:T(4,128)S(1)}, u32[]{:S(2)}, u32[]{:S(2)}) collective-permute-start(f32[3,1536]{1,0:T(4,128)S(1)} %add.314), channel_id=1, source_target_pairs={{0,16},{4,20},{8,24},{12,28},{16,0},{20,4},{24,8},{28,12},{1,17},{... | collective-permute-start | bytes 55304 | tf_op jit(solution)/shard_map/ppermute | solution.py:46
  34.9 3.8 %collective-permute-start.11 = (f32[3,1536]{1,0:T(4,128)S(1)}, f32[3,1536]{1,0:T(4,128)S(1)}, u32[]{:S(2)}, u32[]{:S(2)}) collective-permute-start(f32[3,1536]{1,0:T(4,128)S(1)} %add.314), channel_id=1, source_target_pairs={{0,8},{4,12},{8,0},{12,4},{16,24},{20,28},{24,16},{28,20},{1,9},{5... | collective-permute-start | bytes 55304 | tf_op jit(solution)/shard_map/ppermute | solution.py:46
  38.8 2.4 %copy-start.5 = (f32[3,1536]{1,0:T(4,128)}, f32[3,1536]{1,0:T(4,128)S(1)}, u32[]{:S(2)}) copy-start(f32[3,1536]{1,0:T(4,128)S(1)} %add_multiply_fusion) | copy-start | bytes 55300
  38.9 2.1 %collective-permute-start.14 = (bf16[3,64,1536]{2,1,0:T(8,128)(2,1)S(1)}, bf16[3,64,1536]{2,1,0:T(8,128)(2,1)S(1)}, u32[]{:S(2)}, u32[]{:S(2)}) collective-permute-start(bf16[3,64,1536]{2,1,0:T(8,128)(2,1)S(1)} %subtract_convert_fusion), channel_id=1, source_target_pairs={{0,4},{4,0},{8,12},{12,8},{16,20},{20,16},{24,28},{28,24},{1,5},{5... | collective-permute-start | bytes 1769480 | tf_op jit(solution)/shard_map/ppermute | solution.py:176
  41.4 17.2 %collective-permute-start.17 = (bf16[3,128,768]{2,1,0:T(8,128)(2,1)S(1)}, bf16[3,128,768]{2,1,0:T(8,128)(2,1)S(1)}, u32[]{:S(2)}, u32[]{:S(2)}) collective-permute-start(bf16[3,128,768]{2,1,0:T(8,128)(2,1)S(1)} %get-tuple-element.4.refs_0_), channel_id=1, source_target_pairs={{24,0},{28,4},{16,8},{20,12},{8,16},{12,20},{0,24},{4,28},{25,1},{... | collective-permute-start | bytes 1769480 | tf_op jit(solution)/shard_map/ppermute | solution.py:202
  43.0 27.4 %collective-permute-start.16 = (bf16[3,128,768]{2,1,0:T(8,128)(2,1)S(1)}, bf16[3,128,768]{2,1,0:T(8,128)(2,1)S(1)}, u32[]{:S(2)}, u32[]{:S(2)}) collective-permute-start(bf16[3,128,768]{2,1,0:T(8,128)(2,1)S(1)} %get-tuple-element.4.refs_0_), channel_id=1, source_target_pairs={{16,0},{20,4},{24,8},{28,12},{0,16},{4,20},{8,24},{12,28},{17,1},{... | collective-permute-start | bytes 1769480 | tf_op jit(solution)/shard_map/ppermute | solution.py:202
  43.5 27.0 %collective-permute-start.15 = (bf16[3,128,768]{2,1,0:T(8,128)(2,1)S(1)}, bf16[3,128,768]{2,1,0:T(8,128)(2,1)S(1)}, u32[]{:S(2)}, u32[]{:S(2)}) collective-permute-start(bf16[3,128,768]{2,1,0:T(8,128)(2,1)S(1)} %get-tuple-element.4.refs_0_), channel_id=1, source_target_pairs={{8,0},{12,4},{0,8},{4,12},{24,16},{28,20},{16,24},{20,28},{9,1},{1... | collective-permute-start | bytes 1769480 | tf_op jit(solution)/shard_map/ppermute | solution.py:202
  58.6 53.7 %collective-permute-start.20 = (bf16[3,128,768]{2,1,0:T(8,128)(2,1)S(1)}, bf16[3,128,768]{2,1,0:T(8,128)(2,1)S(1)}, u32[]{:S(2)}, u32[]{:S(2)}) collective-permute-start(bf16[3,128,768]{2,1,0:T(8,128)(2,1)S(1)} %collective-permute-done.17.refs_3_), channel_id=1, source_target_pairs={{0,4},{4,0},{8,12},{12,8},{16,20},{20,16},{24,28},{28,24},{1,5},{5... | collective-permute-start | bytes 1769480 | tf_op jit(solution)/shard_map/ppermute | solution.py:207
  70.4 43.2 %collective-permute-start.19 = (bf16[3,128,768]{2,1,0:T(8,128)(2,1)S(1)}, bf16[3,128,768]{2,1,0:T(8,128)(2,1)}, u32[]{:S(2)}, u32[]{:S(2)}) collective-permute-start(bf16[3,128,768]{2,1,0:T(8,128)(2,1)S(1)} %collective-permute-done.16.refs_2_), channel_id=1, source_target_pairs={{0,4},{4,0},{8,12},{12,8},{16,20},{20,16},{24,28},{28,24},{1,5},{5... | collective-permute-start | bytes 1769480 | tf_op jit(solution)/shard_map/ppermute | solution.py:207
  70.5 48.7 %collective-permute-start.18 = (bf16[3,128,768]{2,1,0:T(8,128)(2,1)S(1)}, bf16[3,128,768]{2,1,0:T(8,128)(2,1)}, u32[]{:S(2)}, u32[]{:S(2)}) collective-permute-start(bf16[3,128,768]{2,1,0:T(8,128)(2,1)S(1)} %collective-permute-done.15.refs_1_), channel_id=1, source_target_pairs={{0,4},{4,0},{8,12},{12,8},{16,20},{20,16},{24,28},{28,24},{1,5},{5... | collective-permute-start | bytes 1769480 | tf_op jit(solution)/shard_map/ppermute | solution.py:207
  71.6 10.8 %collective-permute-start.28 = (bf16[1,128,768]{2,1,0:T(8,128)(2,1)}, bf16[1,128,768]{2,1,0:T(8,128)(2,1)S(1)}, u32[]{:S(2)}, u32[]{:S(2)}) collective-permute-start(bf16[1,128,768]{2,1,0:T(8,128)(2,1)} %slice.665), channel_id=1, source_target_pairs={{16,1},{8,2},{0,3},{12,5},{20,6},{28,7},{17,8},{1,10},{9,11},{13,1... | collective-permute-start | bytes 589832 | tf_op jit(solution)/shard_map/ppermute | solution.py:186
  75.5 11.8 %collective-permute-start.27 = (bf16[1,128,768]{2,1,0:T(8,128)(2,1)}, bf16[1,128,768]{2,1,0:T(8,128)(2,1)S(1)}, u32[]{:S(2)}, u32[]{:S(2)}) collective-permute-start(bf16[1,128,768]{2,1,0:T(8,128)(2,1)} %slice.665), channel_id=1, source_target_pairs={{24,1},{0,2},{8,3},{4,5},{28,6},{20,7},{25,8},{9,10},{1,11},{5,12}... | collective-permute-start | bytes 589832 | tf_op jit(solution)/shard_map/ppermute | solution.py:186
  82.4 0.7 copy-start
  83.0 12.1 %collective-permute-start.26 = (bf16[1,128,768]{2,1,0:T(8,128)(2,1)}, bf16[1,128,768]{2,1,0:T(8,128)(2,1)}, u32[]{:S(2)}, u32[]{:S(2)}) collective-permute-start(bf16[1,128,768]{2,1,0:T(8,128)(2,1)} %slice.665), channel_id=1, source_target_pairs={{0,1},{24,2},{16,3},{28,5},{4,6},{12,7},{1,8},{17,10},{25,11},{29,... | collective-permute-start | bytes 589832 | tf_op jit(solution)/shard_map/ppermute | solution.py:186
  87.3 0.7 copy-start.2
  88.0 22.4 %collective-permute-start.25 = (bf16[1,128,768]{2,1,0:T(8,128)(2,1)}, bf16[1,128,768]{2,1,0:T(8,128)(2,1)}, u32[]{:S(2)}, u32[]{:S(2)}) collective-permute-start(bf16[1,128,768]{2,1,0:T(8,128)(2,1)} %slice.665), channel_id=1, source_target_pairs={{8,1},{16,2},{24,3},{20,5},{12,6},{4,7},{9,8},{25,10},{17,11},{21,... | collective-permute-start | bytes 589832 | tf_op jit(solution)/shard_map/ppermute | solution.py:186
  95.1 33.6 %collective-permute-start.24 = (bf16[2,128,768]{2,1,0:T(8,128)(2,1)S(1)}, bf16[2,128,768]{2,1,0:T(8,128)(2,1)S(1)}, u32[]{:S(2)}, u32[]{:S(2)}) collective-permute-start(bf16[2,128,768]{2,1,0:T(8,128)(2,1)S(1)} %slice.664), channel_id=1, source_target_pairs={{16,1},{8,2},{0,3},{12,5},{20,6},{28,7},{17,8},{1,10},{9,11},{13,1... | collective-permute-start | bytes 1179656 | tf_op jit(solution)/shard_map/ppermute | solution.py:186
  110.4 23.1 %collective-permute-start.23 = (bf16[2,128,768]{2,1,0:T(8,128)(2,1)S(1)}, bf16[2,128,768]{2,1,0:T(8,128)(2,1)S(1)}, u32[]{:S(2)}, u32[]{:S(2)}) collective-permute-start(bf16[2,128,768]{2,1,0:T(8,128)(2,1)S(1)} %slice.664), channel_id=1, source_target_pairs={{24,1},{0,2},{8,3},{4,5},{28,6},{20,7},{25,8},{9,10},{1,11},{5,12}... | collective-permute-start | bytes 1179656 | tf_op jit(solution)/shard_map/ppermute | solution.py:186
  112.3 21.4 %collective-permute-start.22 = (bf16[2,128,768]{2,1,0:T(8,128)(2,1)S(1)}, bf16[2,128,768]{2,1,0:T(8,128)(2,1)S(1)}, u32[]{:S(2)}, u32[]{:S(2)}) collective-permute-start(bf16[2,128,768]{2,1,0:T(8,128)(2,1)S(1)} %slice.664), channel_id=1, source_target_pairs={{0,1},{24,2},{16,3},{28,5},{4,6},{12,7},{1,8},{17,10},{25,11},{29,... | collective-permute-start | bytes 1179656 | tf_op jit(solution)/shard_map/ppermute | solution.py:186
  113.6 29.3 %collective-permute-start.21 = (bf16[2,128,768]{2,1,0:T(8,128)(2,1)S(1)}, bf16[2,128,768]{2,1,0:T(8,128)(2,1)S(1)}, u32[]{:S(2)}, u32[]{:S(2)}) collective-permute-start(bf16[2,128,768]{2,1,0:T(8,128)(2,1)S(1)} %slice.664), channel_id=1, source_target_pairs={{8,1},{16,2},{24,3},{20,5},{12,6},{4,7},{9,8},{25,10},{17,11},{21,... | collective-permute-start | bytes 1179656 | tf_op jit(solution)/shard_map/ppermute | solution.py:186
  119.2 0.9 copy-start.1
  120.1 0.9 copy-start.3
